TPU v7x, 8 devices: a whole 2x2x1 slice. The times are simulated.
8 devices in a mesh: data: 1 (over z), ffn: 2 (over y), hid: 4 (over x, core).
Axes of the slice: x: 2, y: 2, z: 1, core: 2. Of those that a mesh axis runs over, the one named last changes fastest.
Arguments:
- x_in: bfloat16 [64, 4096], P('data', 'hid')
- gain_one: float32 [4096], P('hid')
- gain_two: float32 [4096], P('hid')
- w_gate: bfloat16 [4096, 14336], P('hid', 'ffn')
- w_up: bfloat16 [4096, 14336], P('hid', 'ffn')
- w_down: bfloat16 [14336, 4096], P('ffn', 'hid')
- w_qkv: bfloat16 [4096, 6144], P('hid', 'ffn')
- dx_out: bfloat16 [64, 4096], P('data', 'hid')
- d_qkv: bfloat16 [64, 6144], P('data', 'ffn')
Outputs:
- output 1: bfloat16 [64, 4096], P('data', 'hid')
- output 2: bfloat16 [4096, 14336], P(('data', 'hid'), 'ffn')
- output 3: bfloat16 [4096, 14336], P(('data', 'hid'), 'ffn')
- output 4: bfloat16 [14336, 4096], P(('data', 'ffn'), 'hid')
- output 5: bfloat16 [4096, 6144], P(('data', 'hid'), 'ffn')
- output 6: float32 [4096], P(('data', 'hid'))
- output 7: float32 [4096], P(('data', 'hid'))
All inputs are finite; a program needn't handle non-finite values.
Results may differ from a plain program's by a relative error of at most 0.00512244.
Values are sent between devices in bfloat16 or wider.
A program may use at most 1 GiB of HBM per device.

v0:
```python
import jax
import jax.numpy as jnp
from jax import lax
from jax.sharding import PartitionSpec as P

NORM_EPS = 1e-6


def dot_nt(a_mat, b_mat):
    return lax.dot_general(a_mat, b_mat, (((1,), (1,)), ((), ())), preferred_element_type=jnp.float32)


def dot_tn(a_mat, b_mat):
    return lax.dot_general(a_mat, b_mat, (((0,), (0,)), ((), ())), preferred_element_type=jnp.float32)


def norm_forward(z_val, gain_vec, d_model):
    sq_part = jnp.sum(z_val * z_val, axis=-1, keepdims=True)
    inv_rms = lax.rsqrt(lax.psum(sq_part, "hid") / d_model + NORM_EPS)
    return inv_rms, (z_val * inv_rms * gain_vec).astype(jnp.bfloat16)


def norm_backward(z_val, gain_vec, inv_rms, d_norm, d_model):
    g_dn = gain_vec * d_norm
    dot_tok = lax.psum(jnp.sum(g_dn * z_val, axis=-1, keepdims=True), "hid")
    d_input = inv_rms * g_dn - z_val * (inv_rms ** 3) * (dot_tok / d_model)
    d_gain = jnp.sum(d_norm * z_val * inv_rms, axis=0)
    return d_input, d_gain


def solution(mesh):
    hid_size = mesh.shape["hid"]

    def local_step(x_in, gain_one, gain_two, w_gate, w_up, w_down, w_qkv, dx_out, d_qkv):
        d_model = x_in.shape[1] * hid_size
        x_f32 = x_in.astype(jnp.float32)
        inv_one, normed_one = norm_forward(x_f32, gain_one, d_model)
        gate_part = jnp.dot(normed_one, w_gate, preferred_element_type=jnp.float32)
        up_part = jnp.dot(normed_one, w_up, preferred_element_type=jnp.float32)
        gate_pre, up_pre = lax.psum((gate_part, up_part), "hid")
        gate_silu = jax.nn.silu(gate_pre)
        act_bf = (gate_silu * up_pre).astype(jnp.bfloat16)
        down_sum = lax.psum(jnp.dot(act_bf, w_down, preferred_element_type=jnp.float32), "ffn")
        resid_f32 = (x_f32 + down_sum).astype(jnp.bfloat16).astype(jnp.float32)
        inv_two, normed_two = norm_forward(resid_f32, gain_two, d_model)
        dw_qkv = dot_tn(normed_two, d_qkv).astype(jnp.bfloat16)
        d_normed_two = lax.psum(dot_nt(d_qkv, w_qkv), "ffn")
        d_resid, d_gain_two = norm_backward(resid_f32, gain_two, inv_two, d_normed_two, d_model)
        d_res_tot = dx_out.astype(jnp.float32) + d_resid
        d_res_bf = d_res_tot.astype(jnp.bfloat16)
        dw_down = dot_tn(act_bf, d_res_bf).astype(jnp.bfloat16)
        d_act = lax.psum(dot_nt(d_res_bf, w_down), "hid")
        gate_sig = jax.nn.sigmoid(gate_pre)
        d_gate = (d_act * up_pre * gate_sig * (1.0 + gate_pre * (1.0 - gate_sig))).astype(jnp.bfloat16)
        d_up = (d_act * gate_silu).astype(jnp.bfloat16)
        dw_gate = dot_tn(normed_one, d_gate).astype(jnp.bfloat16)
        dw_up = dot_tn(normed_one, d_up).astype(jnp.bfloat16)
        d_normed_one = lax.psum(dot_nt(d_gate, w_gate) + dot_nt(d_up, w_up), "ffn")
        d_in, d_gain_one = norm_backward(x_f32, gain_one, inv_one, d_normed_one, d_model)
        dx_in = (d_res_tot + d_in).astype(jnp.bfloat16)
        return dx_in, dw_gate, dw_up, dw_down, dw_qkv, d_gain_one, d_gain_two

    tok_spec = P("data", "hid")
    in_specs = (tok_spec, P("hid"), P("hid"), P("hid", "ffn"), P("hid", "ffn"), P("ffn", "hid"), P("hid", "ffn"), tok_spec, P("data", "ffn"))
    out_specs = (tok_spec, P(("data", "hid"), "ffn"), P(("data", "hid"), "ffn"), P(("data", "ffn"), "hid"), P(("data", "hid"), "ffn"), P(("data", "hid")), P(("data", "hid")))
    return jax.shard_map(local_step, mesh=mesh, in_specs=in_specs, out_specs=out_specs, check_vma=False)
```

profile of v0, /device:TPU:0, one launch (start us, length us, event | category | flops | bytes accessed | tf_op | source)
XLA Modules:
  0.0 272.3 jit_solution(3930223125059062205)
XLA Ops:
  7.2 0.0 all-reduce.11.cloned.1.call-start
  7.2 1.1 fusion.10
  8.3 8.8 %psum.70 = f32[64,1]{0,1:T(1,128)S(1)} all-reduce(f32[64,1]{0,1:T(1,128)S(1)} %bitcast.34), channel_id=1, replica_groups=mesh['data'=1,'ffn'=2,'hid'=4] {'hid'}, use_global_device_ids=true, to_apply=%region_1.0 | all-reduce | flops 64 | bytes 512 | tf_op jit(solution)/shard_map/psum | solution.py:19
  17.1 9.4 %fusion.33 = f32[64,7168]{1,0:T(8,128)} fusion(bf16[1024,7168]{1,0:T(8,128)(2,1)} %param.13, bf16[64,1024]{1,0:T(8,128)(2,1)} %param.9, f32[1024]{0:T(1024)} %param.10, f32[64]{0:T(128)S(1)} %get-tuple-element.20), kind=kOutput, calls=%fused_computation.56 | convolution fusion | flops 939786240 | bytes 16650496 | tf_op jit(solution)/shard_map/dot_general | solution.py:39
  26.5 0.7 copy-done.2
  27.1 4.0 %fusion.35 = f32[64,7168]{1,0:T(8,128)} fusion(bf16[1024,7168]{1,0:T(8,128)(2,1)S(1)} %copy-done.2, bf16[64,1024]{1,0:T(8,128)(2,1)S(1)} %copy-done.3, f32[1024]{0:T(1024)S(1)} %copy-done.5, f32[64]{0:T(128)S(1)} %get-tuple-element.20), kind=kOutput, calls=%fused_computation.57 | convolution fusion | flops 939786240 | bytes 16650496 | tf_op jit(solution)/shard_map/dot_general | solution.py:38
  31.1 0.0 all-reduce.13.cloned.1.call-start
  31.2 5.5 %fusion.39 = f32[64,1024]{1,0:T(8,128)} fusion(bf16[64,3072]{1,0:T(8,128)(2,1)S(1)} %copy-done, bf16[1024,3072]{1,0:T(8,128)(2,1)} %param.15), kind=kOutput, calls=%fused_computation.59 | convolution fusion | flops 402653184 | bytes 6946816 | tf_op jit(solution)/shard_map/dot_general | solution.py:10
  36.7 65.9 %all-reduce.11.cloned.1.call-done = (f32[64,7168]{1,0:T(8,128)}, f32[64,7168]{1,0:T(8,128)}) async-done(((f32[64,7168]{1,0:T(8,128)}, f32[64,7168]{1,0:T(8,128)}), (f32[64,7168]{1,0:T(8,128)}, f32[64,7168]{1,0:T(8,128)})) %all-reduce.11.cloned.1.call-update) | async-done | bytes 3670032 | tf_op jit(solution)/shard_map/psum | solution.py:40
  102.6 2.5 multiply_convert_fusion.2
  105.1 8.5 %fusion.38 = f32[64,1024]{1,0:T(8,128)} fusion(bf16[64,7168]{1,0:T(8,128)(2,1)S(1)} %multiply_convert_fusion.2, bf16[7168,1024]{1,0:T(8,128)(2,1)} %param.14), kind=kOutput, calls=%fused_computation.58 | convolution fusion | flops 939524096 | bytes 15859712 | tf_op jit(solution)/shard_map/dot_general | solution.py:43
  113.7 0.0 all-reduce.7.cloned.1.call-start
  113.7 23.1 %all-reduce.13.cloned.1.call-done = (f32[64,1024]{1,0:T(8,128)}, f32[64,1024]{1,0:T(8,128)}) async-done(((f32[64,1024]{1,0:T(8,128)}, f32[64,1024]{1,0:T(8,128)}), (f32[64,1024]{1,0:T(8,128)}, f32[64,1024]{1,0:T(8,128)})) %all-reduce.13.cloned.1.call-update) | async-done | bytes 524304 | tf_op jit(solution)/shard_map/psum | solution.py:43
  136.8 1.1 fusion.1
  138.0 6.3 %psum.74 = f32[64,1]{0,1:T(1,128)S(1)} all-reduce(f32[64,1]{0,1:T(1,128)S(1)} %bitcast.31), channel_id=1, replica_groups=mesh['data'=1,'ffn'=2,'hid'=4] {'hid'}, use_global_device_ids=true, to_apply=%region_6.7 | all-reduce | flops 64 | bytes 512 | tf_op jit(solution)/shard_map/psum | solution.py:19
  144.3 4.6 %convolution_convert_fusion.3 = bf16[1024,3072]{1,0:T(8,128)(2,1)} fusion(bf16[64,3072]{1,0:T(8,128)(2,1)S(1)} %copy-done, bf16[64,1024]{1,0:T(8,128)(2,1)S(1)} %get-tuple-element.16, f32[1024]{0:T(1024)S(1)} %copy-done.7, f32[64]{0:T(128)S(1)} %get-tuple-element.22), kind=kOutput, calls=%fused_computation.3 | convolution fusion | flops 406061056 | bytes 6820096 | tf_op jit(solution)/shard_map/dot_general | solution.py:14
  148.9 0.7 fusion.9
  149.6 6.1 %psum.76 = f32[64,1]{0,1:T(1,128)S(1)} all-reduce(f32[64,1]{0,1:T(1,128)S(1)} %bitcast.32), channel_id=1, replica_groups=mesh['data'=1,'ffn'=2,'hid'=4] {'hid'}, use_global_device_ids=true, to_apply=%region_9.10 | all-reduce | flops 64 | bytes 512 | tf_op jit(solution)/shard_map/psum | solution.py:25
  155.7 0.1 fusion.4
  155.9 11.0 %fusion.25 = f32[64,7168]{1,0:T(8,128)} fusion(bf16[7168,1024]{1,0:T(8,128)(2,1)} %param.14, f32[64,1024]{1,0:T(8,128)S(1)} %fusion.4), kind=kOutput, calls=%fused_computation.44 | convolution fusion | flops 939589632 | bytes 16777216 | tf_op jit(solution)/shard_map/dot_general | solution.py:10
  166.9 0.0 all-reduce.9.cloned.1.call-start
  166.9 7.6 %convolution_convert_fusion = bf16[7168,1024]{1,0:T(8,128)(2,1)} fusion(bf16[64,7168]{1,0:T(8,128)(2,1)S(1)} %multiply_convert_fusion.2, f32[64,1024]{1,0:T(8,128)S(1)} %fusion.4), kind=kOutput, calls=%fused_computation | convolution fusion | flops 946929664 | bytes 15859712 | tf_op jit(solution)/shard_map/dot_general | solution.py:14
  174.5 33.2 %all-reduce.7.cloned.1.call-done = f32[64,7168]{1,0:T(8,128)} async-done(((f32[64,7168]{1,0:T(8,128)}), f32[64,7168]{1,0:T(8,128)}) %all-reduce.7.cloned.1.call-update) | async-done | bytes 1835024 | tf_op jit(solution)/shard_map/psum | solution.py:52
  207.7 2.9 %multiply_convert_fusion = (bf16[64,7168]{1,0:T(8,128)(2,1)S(1)}, bf16[64,7168]{1,0:T(8,128)(2,1)S(1)}) fusion(f32[64,7168]{1,0:T(8,128)} %all-reduce.7.cloned.1.call-done, f32[64,7168]{1,0:T(8,128)} %get-tuple-element.12, f32[64,7168]{1,0:T(8,128)S(1)} %copy-done.4), kind=kLoop, calls=%fused_computation.4 | loop fusion | flops 5963776 | bytes 7340032 | tf_op jit(solution)/shard_map/convert_element_type | solution.py:55
  210.6 9.7 %fusion.40 = f32[64,1024]{1,0:T(8,128)S(1)} fusion(bf16[64,7168]{1,0:T(8,128)(2,1)S(1)} %get-tuple-element.18, bf16[1024,7168]{1,0:T(8,128)(2,1)} %param.12), kind=kOutput, calls=%fused_computation.60 | convolution fusion | flops 939524096 | bytes 15859712 | tf_op jit(solution)/shard_map/dot_general | solution.py:10
  220.4 7.6 %convolution_convert_fusion.2 = bf16[1024,7168]{1,0:T(8,128)(2,1)} fusion(bf16[64,7168]{1,0:T(8,128)(2,1)S(1)} %get-tuple-element.18, bf16[64,1024]{1,0:T(8,128)(2,1)S(1)} %copy-done.3, f32[1024]{0:T(1024)S(1)} %copy-done.5, f32[64]{0:T(128)S(1)} %get-tuple-element.20), kind=kOutput, calls=%fused_computation.2 | convolution fusion | flops 947126272 | bytes 15732992 | tf_op jit(solution)/shard_map/dot_general | solution.py:14
  228.0 10.4 %convolution_add_fusion = f32[64,1024]{1,0:T(8,128)} fusion(f32[64,1024]{1,0:T(8,128)S(1)} %fusion.40, bf16[64,7168]{1,0:T(8,128)(2,1)S(1)} %get-tuple-element.17, bf16[1024,7168]{1,0:T(8,128)(2,1)} %param.13), kind=kOutput, calls=%fused_computation.9 | convolution fusion | flops 939589632 | bytes 16121856 | tf_op jit(solution)/shard_map/dot_general | solution.py:10
  238.5 7.7 %convolution_convert_fusion.1 = bf16[1024,7168]{1,0:T(8,128)(2,1)} fusion(bf16[64,7168]{1,0:T(8,128)(2,1)S(1)} %get-tuple-element.17, bf16[64,1024]{1,0:T(8,128)(2,1)S(1)} %copy-done.3, f32[1024]{0:T(1024)S(1)} %copy-done.5, f32[64]{0:T(128)S(1)} %get-tuple-element.20), kind=kOutput, calls=%fused_computation.1 | convolution fusion | flops 947126272 | bytes 15732992 | tf_op jit(solution)/shard_map/dot_general | solution.py:14
  246.1 10.1 %all-reduce.9.cloned.1.call-done = f32[64,1024]{1,0:T(8,128)} async-done(((f32[64,1024]{1,0:T(8,128)}), f32[64,1024]{1,0:T(8,128)}) %all-reduce.9.cloned.1.call-update) | async-done | bytes 262160 | tf_op jit(solution)/shard_map/psum | solution.py:58
  256.2 1.6 fusion.20
  257.9 6.2 %psum.79 = f32[64,1]{0,1:T(1,128)S(1)} all-reduce(f32[64,1]{0,1:T(1,128)S(1)} %bitcast.33), channel_id=1, replica_groups=mesh['data'=1,'ffn'=2,'hid'=4] {'hid'}, use_global_device_ids=true, to_apply=%region_13.14 | all-reduce | flops 64 | bytes 512 | tf_op jit(solution)/shard_map/psum | solution.py:25
  264.0 1.7 fusion.17
  (25 shorter events, 0.1 us)
Async XLA Ops:
  7.2 24.0 %copy-start = (bf16[64,3072]{1,0:T(8,128)(2,1)S(1)}, bf16[64,3072]{1,0:T(8,128)(2,1)}, u32[]{:S(2)}) copy-start(bf16[64,3072]{1,0:T(8,128)(2,1)} %param.17) | copy-start | bytes 1179652
  7.2 95.4 %all-reduce.11.cloned.1.call-start = ((), (), s32[]{:S(2)}) async-start(), calls=%async_computation.2 | async-start | bytes 7340032 | tf_op jit(solution)/shard_map/psum | solution.py:40
  17.1 10.1 %copy-start.2 = (bf16[1024,7168]{1,0:T(8,128)(2,1)S(1)}, bf16[1024,7168]{1,0:T(8,128)(2,1)}, u32[]{:S(2)}) copy-start(bf16[1024,7168]{1,0:T(8,128)(2,1)} %param.12) | copy-start | bytes 44040196
  17.1 10.1 %copy-start.3 = (bf16[64,1024]{1,0:T(8,128)(2,1)S(1)}, bf16[64,1024]{1,0:T(8,128)(2,1)}, u32[]{:S(2)}) copy-start(bf16[64,1024]{1,0:T(8,128)(2,1)} %param.9) | copy-start | bytes 393220
  17.1 10.1 %copy-start.5 = (f32[1024]{0:T(1024)S(1)}, f32[1024]{0:T(1024)}, u32[]{:S(2)}) copy-start(f32[1024]{0:T(1024)} %param.10) | copy-start | bytes 12292
  31.1 105.7 %all-reduce.13.cloned.1.call-start = ((), (), s32[]{:S(2)}) async-start(), calls=%async_computation.3 | async-start | bytes 1048576 | tf_op jit(solution)/shard_map/psum | solution.py:43
  105.1 39.2 %copy-start.7 = (f32[1024]{0:T(1024)S(1)}, f32[1024]{0:T(1024)}, u32[]{:S(2)}) copy-start(f32[1024]{0:T(1024)} %param.11) | copy-start | bytes 12292
  113.7 42.0 %copy-start.8 = (bf16[64,1024]{1,0:T(8,128)(2,1)S(1)}, bf16[64,1024]{1,0:T(8,128)(2,1)}, u32[]{:S(2)}) copy-start(bf16[64,1024]{1,0:T(8,128)(2,1)} %param.16) | copy-start | bytes 393220
  113.7 94.0 %all-reduce.7.cloned.1.call-start = ((), (), s32[]{:S(2)}) async-start(), calls=%async_computation | async-start | bytes 3670016 | tf_op jit(solution)/shard_map/psum | solution.py:52
  136.8 12.1 %copy-start.6 = (f32[64,1024]{1,0:T(8,128)S(1)}, f32[64,1024]{1,0:T(8,128)}, u32[]{:S(2)}) copy-start(f32[64,1024]{1,0:T(8,128)} %get-tuple-element.14) | copy-start | bytes 786436
  166.8 40.9 %copy-start.4 = (f32[64,7168]{1,0:T(8,128)S(1)}, f32[64,7168]{1,0:T(8,128)}, u32[]{:S(2)}) copy-start(f32[64,7168]{1,0:T(8,128)} %get-tuple-element.11) | copy-start | bytes 5505028
  166.9 89.3 %all-reduce.9.cloned.1.call-start = ((), (), s32[]{:S(2)}) async-start(), calls=%async_computation.1 | async-start | bytes 524288 | tf_op jit(solution)/shard_map/psum | solution.py:58
  238.5 27.3 %copy-start.1 = (bf16[64,3072]{1,0:T(8,128)(2,1)S(1)}, bf16[64,3072]{1,0:T(8,128)(2,1)}, u32[]{:S(2)}) copy-start(bf16[64,3072]{1,0:T(8,128)(2,1)} %param.17) | copy-start | bytes 1179652
Sparse Core Ops, SparseCore 0:
  31.3 71.2 all-reduce.10
  113.8 22.9 all-reduce.12
  167.0 40.7 all-reduce.6
  238.6 17.5 all-reduce.8
where the time goes:
time: 273 us; the launch traced here: 272 us
  waiting for transfers between devices  132 us (48%)
  matrix products  86 us (32%)
  blocking collectives  27.3 us (10%)
  between operations  13.9 us (5%)
  other arithmetic  11.9 us (4%)
    psum x1, waiting for transfers between devices, local_step(): gate_pre, up_pre = lax.psum((gate_part, up_part), 'hid')  65.9 us
    dot_general x4, matrix products, dot_nt(): lax.dot_general(a_mat, b_mat, (((1,), (1,)), ((), ())), preferred_element...  36.6 us
    psum x1, waiting for transfers between devices, local_step(): d_act = lax.psum(dot_nt(d_res_bf, w_down), 'hid')  33.2 us
    dot_general x4, matrix products, dot_tn(): lax.dot_general(a_mat, b_mat, (((0,), (0,)), ((), ())), preferred_element...  27.5 us
    psum x1, waiting for transfers between devices, local_step(): lax.psum(jnp.dot(act_bf, w_down, preferred_element_type=jnp.float32), 'ffn')  23.1 us
    psum x2, blocking collectives, norm_forward(): inv_rms = lax.rsqrt(lax.psum(sq_part, 'hid') / d_model + NORM_EPS)  15.1 us
    psum x2, blocking collectives, norm_backward(): dot_tok = lax.psum(jnp.sum(g_dn * z_val, axis=-1, keepdims=True), 'hid')  12.3 us
    psum x1, waiting for transfers between devices, local_step(): d_normed_one = lax.psum(dot_nt(d_gate, w_gate) + dot_nt(d_up, w_up), 'ffn')  10.1 us
  transfers between devices with their start and end apart: 4, of which 4 were waited for; matrix products, arithmetic and copies ran while one was open for 8% of the time, Pallas kernels for 0%

commit v1 on v0

v1 whole, which is shorter than its diff:
```python
import functools

import jax
import jax.numpy as jnp
from jax import lax
from jax.experimental import pallas as pl
from jax.experimental.pallas import tpu as pltpu
from jax.sharding import PartitionSpec as P

NORM_EPS = 1e-6
BF = jnp.bfloat16
F32 = jnp.float32
MESH_ID = pl.DeviceIdType.MESH
ANY = pl.BlockSpec(memory_space=pl.ANY)
VMEM_LIMIT = 67043328

CHUNK = 1024
LAG_PAIR = 1
LAG_ACT = 2
LAG_FWD = 3
LAG_DOT = 4

PAIR, XRED, GX, GP, FW = range(5)


def nn_dot(a_mat, b_mat):
    return jnp.dot(a_mat, b_mat, preferred_element_type=F32)


def nt_dot(a_mat, b_mat):
    return lax.dot_general(a_mat, b_mat, (((1,), (1,)), ((), ())), preferred_element_type=F32)


def pack_stats(cols):
    tok = cols[0].shape[0]
    lane = lax.broadcasted_iota(jnp.int32, (tok, 128), 1)
    wide = jnp.zeros((tok, 128), F32)
    for i, col in enumerate(cols):
        wide = jnp.where(lane == i, col, wide)
    full = jnp.concatenate([wide, jnp.zeros((128 - tok, 128), F32)], axis=0)
    return full.T[0:8, :]


def unpack_stats(tile, tok, count):
    full = jnp.concatenate([tile, jnp.zeros((120, 128), F32)], axis=0).T
    return [full[0:tok, i : i + 1] for i in range(count)]


def comm_kernel(
    dims,
    x_h, g1_h, g2_h, wg_h, wu_h, wd_h, wq_h, dx_h, dq_h,
    n1_o, n2_o, eb_o, a_o, dgu_o, dxin_o, dg1_o, dg2_o,
    wg, wu, wd, wq, dq, x_s, dx_s, g1, g2, n1, n2, eb, e_s, x2_s,
    acc, part, r1, r2, xs, xr, xs2, xr2, gu, a_f, dgu_f, ys, yr, st_s, st_r, dxin_s, dg_s,
    ld, wld, out_sem, st_sem, y_sem, sems,
):
    tok, hd, ff, qw = dims
    c_w = CHUNK
    nc = ff // c_w
    half = c_w // 2
    quart = c_w // 4
    d_model = hd * 4
    zc, yc, h = lax.axis_index("data"), lax.axis_index("ffn"), lax.axis_index("hid")
    xc = h // 2
    core = lax.rem(h, 2)
    pair = (zc, yc, xc * 2 + 1 - core)
    xnb = (zc, yc, (1 - xc) * 2 + core)
    ynb = (zc, 1 - yc, h)

    def load(src, dst, sem):
        return pltpu.make_async_copy(src, dst, sem)

    small = [
        load(x_h, x_s, ld.at[0]), load(g1_h, g1, ld.at[1]), load(dq_h, dq, ld.at[2]),
        load(g2_h, g2, ld.at[3]), load(dx_h, dx_s, ld.at[4]),
    ]
    qn = qw // 1024

    def wq_load(i):
        cols = pl.ds(pl.multiple_of(i * 1024, 1024), 1024)
        return load(wq_h.at[:, cols], wq.at[:, cols], wld.at[3, i])

    def w_load(i, c):
        cols = pl.ds(pl.multiple_of(c * c_w, c_w), c_w)
        if i == 2:
            return load(wd_h.at[cols, :], wd.at[cols, :], wld.at[2, c])
        src, dst = ((wg_h, wg), (wu_h, wu))[i]
        return load(src.at[:, cols], dst.at[:, cols], wld.at[i, c])

    for cp in small:
        cp.start()
    for i in range(qn):
        wq_load(i).start()
    for c in range(nc):
        w_load(0, c).start()
        w_load(1, c).start()
    for c in range(nc):
        w_load(2, c).start()

    bar = pltpu.get_barrier_semaphore()
    for j in (1, 2, 3):
        pl.semaphore_signal(bar, inc=1, device_id=(zc, yc, lax.rem(h + j, 4)), device_id_type=MESH_ID)
    pl.semaphore_signal(bar, inc=1, device_id=ynb, device_id_type=MESH_ID)
    pl.semaphore_wait(bar, 4)

    def stat_copy(n, j):
        return pltpu.make_async_remote_copy(
            src_ref=st_s.at[n], dst_ref=st_r.at[n, h], send_sem=st_sem.at[n, 0, j], recv_sem=st_sem.at[n, 1, j],
            device_id=(zc, yc, lax.rem(h + j, 4)), device_id_type=MESH_ID,
        )

    def stat_send(n, cols):
        tile = pack_stats(cols)
        st_s[n] = tile
        st_r[n, h] = tile
        for j in (1, 2, 3):
            stat_copy(n, j).start()

    def stat_recv(n, count):
        for j in (1, 2, 3):
            stat_copy(n, j).wait()
        return unpack_stats(st_r[n, 0] + st_r[n, 1] + st_r[n, 2] + st_r[n, 3], tok, count)

    def y_copy(n):
        return pltpu.make_async_remote_copy(
            src_ref=ys.at[n], dst_ref=yr.at[n], send_sem=y_sem.at[n, 0], recv_sem=y_sem.at[n, 1],
            device_id=ynb, device_id_type=MESH_ID,
        )

    def y_sum(n):
        y_copy(n).wait()
        return ys[n].astype(F32) + yr[n].astype(F32)

    small[0].wait()
    x_f = x_s[...].astype(F32)
    stat_send(0, [jnp.sum(x_f * x_f, axis=-1, keepdims=True)])
    small[2].wait()
    acc[...] = jnp.zeros_like(acc)

    def qkv_step(i, carry):
        wq_load(i).wait()
        cols = pl.ds(pl.multiple_of(i * 1024, 1024), 1024)
        acc[...] += nt_dot(dq[:, cols], wq[:, cols])
        return carry

    lax.fori_loop(0, qn, qkv_step, 0)
    ys[0] = acc[...].astype(BF)
    y_copy(0).start()
    small[1].wait()
    (sq,) = stat_recv(0, 1)
    inv1 = lax.rsqrt(sq / d_model + NORM_EPS)
    n1[...] = (x_s[...].astype(F32) * inv1 * g1[...]).astype(BF)
    n1_out = load(n1, n1_o, out_sem.at[0])
    n1_out.start()
    acc[...] = jnp.zeros_like(acc)

    def pair_copy(ph, c):
        slot = lax.rem(c, 2)
        src = part.at[slot, 1 - core] if ph == 0 else part.at[slot, 1 - core, 0]
        return pltpu.make_async_remote_copy(
            src_ref=src, dst_ref=(r1 if ph == 0 else r2).at[c],
            send_sem=sems.at[ph, 2 * PAIR, c], recv_sem=sems.at[ph, 2 * PAIR + 1, c],
            device_id=pair, device_id_type=MESH_ID,
        )

    def x_copy(ph, c):
        src, dst = ((xs, xr), (xs2, xr2))[ph]
        return pltpu.make_async_remote_copy(
            src_ref=src.at[c], dst_ref=dst.at[c],
            send_sem=sems.at[ph, 2 * XRED, c], recv_sem=sems.at[ph, 2 * XRED + 1, c],
            device_id=xnb, device_id_type=MESH_ID,
        )

    own_q = core * 2 + xc
    xnb_q = core * 2 + 1 - xc

    def block(ph, c, q):
        cols = pl.ds(pl.multiple_of(c * c_w + q * quart, quart), quart)
        return a_f.at[:, cols] if ph == 0 else dgu_f.at[:, :, cols]

    def g_copy(ph, c, kind):
        ref = block(ph, c, xnb_q if kind == FW else own_q)
        return pltpu.make_async_remote_copy(
            src_ref=ref, dst_ref=ref,
            send_sem=sems.at[ph, 2 * kind, c], recv_sem=sems.at[ph, 2 * kind + 1, c],
            device_id=xnb if kind == GX else pair, device_id_type=MESH_ID,
        )

    own_cols = pl.ds(pl.multiple_of(xc * quart, quart), quart)
    oth_cols = pl.ds(pl.multiple_of((1 - xc) * quart, quart), quart)

    def pipeline(ph, partial, activate, consume):
        def step(t, carry):
            @pl.when(t < nc)
            def _():
                c = t

                @pl.when(c >= 2)
                def _():
                    pair_copy(ph, c - 2).wait_send()

                partial(c, 1 - core)
                pair_copy(ph, c).start()
                partial(c, core)

            @pl.when((t >= LAG_PAIR) & (t < nc + LAG_PAIR))
            def _():
                c = t - LAG_PAIR
                slot = lax.rem(c, 2)
                pair_copy(ph, c).wait_recv()
                if ph == 0:
                    xs[c] = (part[slot, core, :, :, oth_cols] + r1[c, :, :, oth_cols]).astype(BF)
                    x_copy(ph, c).start()
                    gu[c] = part[slot, core, :, :, own_cols] + r1[c, :, :, own_cols]
                else:
                    xs2[c] = (part[slot, core, 0, :, oth_cols] + r2[c, :, oth_cols]).astype(BF)
                    x_copy(ph, c).start()
                    r2[c, :, own_cols] = part[slot, core, 0, :, own_cols] + r2[c, :, own_cols]

            @pl.when((t >= LAG_ACT) & (t < nc + LAG_ACT))
            def _():
                c = t - LAG_ACT
                x_copy(ph, c).wait_recv()
                activate(c)
                g_copy(ph, c, GX).start()
                g_copy(ph, c, GP).start()

            @pl.when((t >= LAG_FWD) & (t < nc + LAG_FWD))
            def _():
                c = t - LAG_FWD
                g_copy(ph, c, GX).wait_recv()
                g_copy(ph, c, FW).start()

            @pl.when((t >= LAG_DOT) & (t < nc + LAG_DOT))
            def _():
                c = t - LAG_DOT
                g_copy(ph, c, GP).wait_recv()
                g_copy(ph, c, FW).wait_recv()
                consume(c)
                x_copy(ph, c).wait_send()
                g_copy(ph, c, GX).wait_send()
                g_copy(ph, c, GP).wait_send()
                g_copy(ph, c, FW).wait_send()

            return carry

        lax.fori_loop(0, nc + LAG_DOT, step, 0)
        pair_copy(ph, nc - 2).wait_send()
        pair_copy(ph, nc - 1).wait_send()

    def gu_partial(c, which):
        @pl.when(which != core)
        def _():
            w_load(0, c).wait()
            w_load(1, c).wait()

        cols = pl.ds(pl.multiple_of(c * c_w + which * half, half), half)
        slot = lax.rem(c, 2)
        part[slot, which, 0] = nn_dot(n1[...], wg[:, cols])
        part[slot, which, 1] = nn_dot(n1[...], wu[:, cols])

    def act_forward(c):
        gate = gu[c, 0] + xr[c, 0].astype(F32)
        up = gu[c, 1] + xr[c, 1].astype(F32)
        gu[c, 0] = gate
        gu[c, 1] = up
        cols = pl.ds(pl.multiple_of(c * c_w + own_q * quart, quart), quart)
        a_f[:, cols] = (jax.nn.silu(gate) * up).astype(BF)

    def down_dot(c):
        w_load(2, c).wait()
        rows = pl.ds(pl.multiple_of(c * c_w, c_w), c_w)
        acc[...] += nn_dot(a_f[:, rows], wd[rows, :])

    pipeline(0, gu_partial, act_forward, down_dot)
    ys[1] = acc[...].astype(BF)
    y_copy(1).start()
    a_out = load(a_f, a_o, out_sem.at[1])
    a_out.start()

    small[3].wait()
    small[4].wait()
    dn2 = y_sum(0)
    acc[...] = dn2
    x2_s[...] = (x_s[...].astype(F32) + y_sum(1)).astype(BF)
    x2 = x2_s[...].astype(F32)
    stat_send(1, [
        jnp.sum(x2 * x2, axis=-1, keepdims=True),
        jnp.sum(g2[...] * acc[...] * x2, axis=-1, keepdims=True),
    ])
    sq2, dot2 = stat_recv(1, 2)
    inv2 = lax.rsqrt(sq2 / d_model + NORM_EPS)
    x2 = x2_s[...].astype(F32)
    dz2 = inv2 * (g2[...] * acc[...]) - x2 * (inv2 * inv2 * inv2) * (dot2 / d_model)
    e_val = dx_s[...].astype(F32) + dz2
    e_s[...] = e_val
    eb[...] = e_val.astype(BF)
    n2[...] = (x2_s[...].astype(F32) * inv2 * g2[...]).astype(BF)
    dg_s[0:1, :] = jnp.sum(acc[...] * x2_s[...].astype(F32) * inv2, axis=0, keepdims=True)
    outs = [load(eb, eb_o, out_sem.at[2]), load(n2, n2_o, out_sem.at[3])]
    for cp in outs:
        cp.start()
    acc[...] = jnp.zeros_like(acc)

    def da_partial(c, which):
        rows = pl.ds(pl.multiple_of(c * c_w + which * half, half), half)
        part[lax.rem(c, 2), which, 0] = nt_dot(eb[...], wd[rows, :])

    def act_backward(c):
        d_act = r2[c, :, own_cols] + xr2[c].astype(F32)
        gate, up = gu[c, 0], gu[c, 1]
        sig = jax.nn.sigmoid(gate)
        cols = pl.ds(pl.multiple_of(c * c_w + own_q * quart, quart), quart)
        dgu_f[0, :, cols] = (d_act * up * sig * (1.0 + gate * (1.0 - sig))).astype(BF)
        dgu_f[1, :, cols] = (d_act * (gate * sig)).astype(BF)

    def dn1_dot(c):
        cols = pl.ds(pl.multiple_of(c * c_w, c_w), c_w)
        acc[...] += nt_dot(dgu_f[0, :, cols], wg[:, cols]) + nt_dot(dgu_f[1, :, cols], wu[:, cols])

    pipeline(1, da_partial, act_backward, dn1_dot)
    dgu_out = load(dgu_f, dgu_o, out_sem.at[4])
    dgu_out.start()
    ys[2] = acc[...].astype(BF)
    y_copy(2).start()

    acc[...] = y_sum(2)
    stat_send(2, [jnp.sum(g1[...] * acc[...] * x_s[...].astype(F32), axis=-1, keepdims=True)])
    dg_s[1:2, :] = jnp.sum(acc[...] * x_s[...].astype(F32) * inv1, axis=0, keepdims=True)
    (dot1,) = stat_recv(2, 1)
    dz1 = inv1 * (g1[...] * acc[...]) - x_s[...].astype(F32) * (inv1 * inv1 * inv1) * (dot1 / d_model)
    dxin_s[...] = (e_s[...] + dz1).astype(BF)
    tail = [
        load(dxin_s, dxin_o, out_sem.at[5]),
        load(dg_s.at[0:1, :], dg2_o, out_sem.at[6]),
        load(dg_s.at[1:2, :], dg1_o, out_sem.at[7]),
    ]
    for cp in tail:
        cp.start()
    for cp in (n1_out, a_out, *outs, dgu_out, *tail):
        cp.wait()


def comm_call(x_in, gain_one, gain_two, w_gate, w_up, w_down, w_qkv, dx_out, d_qkv):
    tok, hd = x_in.shape
    ff = w_gate.shape[1]
    qw = w_qkv.shape[1]
    nc = ff // CHUNK
    half, quart = CHUNK // 2, CHUNK // 4
    out = lambda shape, dtype: jax.ShapeDtypeStruct(shape, dtype)
    vm = lambda *shape_dtype: pltpu.VMEM(shape_dtype[:-1], shape_dtype[-1])
    dma = pltpu.SemaphoreType.DMA
    return pl.pallas_call(
        functools.partial(comm_kernel, (tok, hd, ff, qw)),
        out_shape=(
            out((tok, hd), BF), out((tok, hd), BF), out((tok, hd), BF), out((tok, ff), BF), out((2, tok, ff), BF),
            out((tok, hd), BF), out((1, hd), F32), out((1, hd), F32),
        ),
        in_specs=[ANY] * 9,
        out_specs=[ANY] * 8,
        scratch_shapes=[
            vm(hd, ff, BF), vm(hd, ff, BF), vm(ff, hd, BF), vm(hd, qw, BF), vm(tok, qw, BF),
            vm(tok, hd, BF), vm(tok, hd, BF), vm(1, hd, F32), vm(1, hd, F32),
            vm(tok, hd, BF), vm(tok, hd, BF), vm(tok, hd, BF), vm(tok, hd, F32), vm(tok, hd, BF),
            vm(tok, hd, F32), vm(2, 2, 2, tok, half, F32), vm(nc, 2, tok, half, F32), vm(nc, tok, half, F32),
            vm(nc, 2, tok, quart, BF), vm(nc, 2, tok, quart, BF), vm(nc, tok, quart, BF), vm(nc, tok, quart, BF),
            vm(nc, 2, tok, quart, F32), vm(tok, ff, BF), vm(2, tok, ff, BF),
            vm(3, tok, hd, BF), vm(3, tok, hd, BF), vm(3, 8, 128, F32), vm(3, 4, 8, 128, F32),
            vm(tok, hd, BF), vm(8, hd, F32),
            dma((5,)), dma((4, nc)), dma((8,)), dma((3, 2, 4)), dma((3, 2)), dma((2, 10, nc)),
        ],
        compiler_params=pltpu.CompilerParams(
            collective_id=0, has_side_effects=True, vmem_limit_bytes=VMEM_LIMIT
        ),
        name="block_comm",
    )(x_in, gain_one, gain_two, w_gate, w_up, w_down, w_qkv, dx_out, d_qkv)


TILE = 512
SLOTS = 3


def grad_kernel(dims, n1, n2, eb, a_f, dgu, dq, dwg_o, dwu_o, dwd_o, dwq_o, n1_t, n2_t, bg, bu, bd, sem):
    hd, ff, qw = dims
    nt, nq = ff // TILE, qw // TILE
    n1_t[...] = n1[...].astype(F32).T.astype(BF)
    n2_t[...] = n2[...].astype(F32).T.astype(BF)

    def cols_of(i):
        return pl.ds(pl.multiple_of(i * TILE, TILE), TILE)

    def q_copy(i):
        slot = lax.rem(i, SLOTS)
        return pltpu.make_async_copy(bg.at[slot], dwq_o.at[:, cols_of(i)], sem.at[0, slot])

    def g_copy(i):
        slot = lax.rem(i, SLOTS)
        return pltpu.make_async_copy(bg.at[slot], dwg_o.at[:, cols_of(i)], sem.at[0, slot])

    def u_copy(i):
        slot = lax.rem(i, SLOTS)
        return pltpu.make_async_copy(bu.at[slot], dwu_o.at[:, cols_of(i)], sem.at[1, slot])

    def d_copy(i):
        slot = lax.rem(i, SLOTS)
        return pltpu.make_async_copy(bd.at[slot], dwd_o.at[cols_of(i), :], sem.at[2, slot])

    def q_step(i, carry):
        @pl.when(i >= SLOTS)
        def _():
            q_copy(i - SLOTS).wait()

        bg[lax.rem(i, SLOTS)] = nn_dot(n2_t[...], dq[:, cols_of(i)]).astype(BF)
        q_copy(i).start()
        return carry

    lax.fori_loop(0, nq, q_step, 0)
    for i in range(nq - SLOTS, nq):
        q_copy(i).wait()

    def step(i, carry):
        slot = lax.rem(i, SLOTS)

        @pl.when(i >= SLOTS)
        def _():
            g_copy(i - SLOTS).wait()
            u_copy(i - SLOTS).wait()
            d_copy(i - SLOTS).wait()

        bd[slot] = nn_dot(a_f[:, cols_of(i)].astype(F32).T.astype(BF), eb[...]).astype(BF)
        d_copy(i).start()
        bg[slot] = nn_dot(n1_t[...], dgu[0, :, cols_of(i)]).astype(BF)
        g_copy(i).start()
        bu[slot] = nn_dot(n1_t[...], dgu[1, :, cols_of(i)]).astype(BF)
        u_copy(i).start()
        return carry

    lax.fori_loop(0, nt, step, 0)
    for i in range(nt - SLOTS, nt):
        g_copy(i).wait()
        u_copy(i).wait()
        d_copy(i).wait()


def grad_call(n1, n2, eb, a_full, dgu, d_qkv):
    tok, hd = n1.shape
    ff, qw = a_full.shape[1], d_qkv.shape[1]
    out = lambda *shape: jax.ShapeDtypeStruct(shape, BF)
    return pl.pallas_call(
        functools.partial(grad_kernel, (hd, ff, qw)),
        out_shape=(out(hd, ff), out(hd, ff), out(ff, hd), out(hd, qw)),
        in_specs=[pl.BlockSpec(memory_space=pltpu.VMEM)] * 6,
        out_specs=[ANY] * 4,
        scratch_shapes=[
            pltpu.VMEM((hd, tok), BF), pltpu.VMEM((hd, tok), BF),
            pltpu.VMEM((SLOTS, hd, TILE), BF), pltpu.VMEM((SLOTS, hd, TILE), BF), pltpu.VMEM((SLOTS, TILE, hd), BF),
            pltpu.SemaphoreType.DMA((3, SLOTS)),
        ],
        compiler_params=pltpu.CompilerParams(vmem_limit_bytes=VMEM_LIMIT),
        name="weight_grads",
    )(n1, n2, eb, a_full, dgu, d_qkv)


def solution(mesh):
    def local_step(x_in, gain_one, gain_two, w_gate, w_up, w_down, w_qkv, dx_out, d_qkv):
        hd = x_in.shape[1]
        n1, n2, eb, a_full, dgu, dx_in, dg1, dg2 = comm_call(
            x_in, gain_one.reshape(1, hd), gain_two.reshape(1, hd), w_gate, w_up, w_down, w_qkv, dx_out, d_qkv
        )
        dw_gate, dw_up, dw_down, dw_qkv = grad_call(n1, n2, eb, a_full, dgu, d_qkv)
        return dx_in, dw_gate, dw_up, dw_down, dw_qkv, dg1.reshape(hd), dg2.reshape(hd)

    tok_spec = P("data", "hid")
    in_specs = (tok_spec, P("hid"), P("hid"), P("hid", "ffn"), P("hid", "ffn"), P("ffn", "hid"), P("hid", "ffn"), tok_spec, P("data", "ffn"))
    out_specs = (tok_spec, P(("data", "hid"), "ffn"), P(("data", "hid"), "ffn"), P(("data", "ffn"), "hid"), P(("data", "hid"), "ffn"), P(("data", "hid")), P(("data", "hid")))
    return jax.shard_map(local_step, mesh=mesh, in_specs=in_specs, out_specs=out_specs, check_vma=False)
```

time: 273 us -> 114 us (0.42)
  waiting for transfers between devices: 132 us -> 0 us
  Pallas kernels: 0 us -> 109 us
  matrix products: 86 us -> 0 us
  blocking collectives: 27.3 us -> 0 us
  between operations: 13.9 us -> 0.65 us
  other arithmetic: 11.9 us -> 0 us
  local copies, waits for them, and re-layouts: 0.73 us -> 4.11 us
    psum x4 -> x0, waiting for transfers between devices: 132 us -> none  [the longest x1 65.9 us: local_step(): gate_pre, up_pre = lax.psum((gate_part, up_part), 'hid')]
    pallas_call x0 -> x2, Pallas kernels: none -> 109 us  [the longest x1 87.7 us: comm_call(): pl.pallas_call(functools.partial(comm_kernel, (tok, hd, ff, qw)), out_sha...]
    dot_general x11 -> x0, matrix products: 86 us -> none  [the longest x4 36.6 us: dot_nt(): lax.dot_general(a_mat, b_mat, (((1,), (1,)), ((), ())), preferred_element...]
    psum x4 -> x0, blocking collectives: 27.3 us -> none  [the longest x2 15.1 us: norm_forward(): inv_rms = lax.rsqrt(lax.psum(sq_part, 'hid') / d_model + NORM_EPS)]
    convert_element_type x3 -> x0, other arithmetic: 7.17 us -> none  [the longest x1 2.9 us: local_step(): d_up = (d_act * gate_silu).astype(jnp.bfloat16)]
    reduce_sum x4 -> x0, other arithmetic: 4.54 us -> none  [the longest x2 2.34 us: norm_backward(): d_gain = jnp.sum(d_norm * z_val * inv_rms, axis=0)]
    unnamed x18 -> x3, local copies, waits for them, and re-layouts: 0.73 us -> 4.11 us
  transfers between devices with their start and end apart: 4 -> 0, of which waited for: 4 -> 0; matrix products, arithmetic and copies ran while one was open for 8% -> 0% of each run, Pallas kernels for 0% -> 0%
where the time goes in v1:
time: 114 us
  Pallas kernels  109 us (96%)
  local copies, waits for them, and re-layouts  4.11 us (4%)
    pallas_call x1, Pallas kernels, comm_call(): pl.pallas_call(functools.partial(comm_kernel, (tok, hd, ff, qw)), out_sha...  87.7 us
    pallas_call x1, Pallas kernels, grad_call(): pl.pallas_call(functools.partial(grad_kernel, (hd, ff, qw)), out_shape=(o...  21.4 us
    unnamed x3, local copies, waits for them, and re-layouts  4.11 us

profile of v1, /device:TPU:0, one launch (start us, length us, event | category | flops | bytes accessed | tf_op | source)
XLA Modules:
  0.0 113.9 jit_solution(9001267848140319938)
XLA Ops:
  0.6 87.7 %block_comm.1 = (bf16[64,1024]{1,0:T(8,128)(2,1)}, bf16[64,1024]{1,0:T(8,128)(2,1)}, bf16[64,1024]{1,0:T(8,128)(2,1)}, bf16[64,7168]{1,0:T(8,128)(2,1)}, bf16[2,...) custom-call(bf16[64,1024]{1,0:T(8,128)(2,1)} %x_h.1, ...), custom_call_target="tpu_custom_call" | custom-call | tf_op jit(solution)/shard_map/block_comm/pallas_call | solution.py:353
  88.3 21.4 %weight_grads.1 = (bf16[1024,7168]{1,0:T(8,128)(2,1)}, bf16[1024,7168]{1,0:T(8,128)(2,1)}, bf16[7168,1024]{1,0:T(8,128)(2,1)}, bf16[1024,3072]{1,0:T(8,128)(2,1)}) custom-call(bf16[64,1024]{1,0:T(8,128)(2,1)} %get-tuple-element.20.n1, bf16[64,1024]{1,0:T(8,128)(2,1)} %get-tuple-element.21.n2, bf16[64,1024]{1,0:T(8,128)(2,1)} %get-tuple-element.22.eb, ...), custom_call_target="tpu_custom_call" | custom-call | tf_op jit(solution)/shard_map/weight_grads/pallas_call | solution.py:449
  109.8 1.6 %copy.19 = bf16[64,1024]{1,0:T(8,128)(2,1)} copy(bf16[64,1024]{1,0:T(8,128)(2,1)} %get-tuple-element.38) | data formatting | bytes 262144
  111.3 1.3 %copy.20 = f32[1024]{0:T(1024)} copy(f32[1024]{0:T(1024)} %bitcast.5) | data formatting | bytes 8192
  112.6 1.3 %copy.21 = f32[1024]{0:T(1024)} copy(f32[1024]{0:T(1024)} %bitcast.4) | data formatting | bytes 8192

commit v2 on v1

--- a/solution.py
+++ b/solution.py
@@ -15,10 +15,7 @@
 VMEM_LIMIT = 67043328
 
 CHUNK = 1024
-LAG_PAIR = 1
-LAG_ACT = 2
-LAG_FWD = 3
-LAG_DOT = 4
+LAGS = ((1, 3, 5, 6), (1, 3, 5, 6))
 
 PAIR, XRED, GX, GP, FW = range(5)
 
@@ -51,7 +48,7 @@
     x_h, g1_h, g2_h, wg_h, wu_h, wd_h, wq_h, dx_h, dq_h,
     n1_o, n2_o, eb_o, a_o, dgu_o, dxin_o, dg1_o, dg2_o,
     wg, wu, wd, wq, dq, x_s, dx_s, g1, g2, n1, n2, eb, e_s, x2_s,
-    acc, part, r1, r2, xs, xr, xs2, xr2, gu, a_f, dgu_f, ys, yr, st_s, st_r, dxin_s, dg_s,
+    acc, part, r1, r2, xs, xr, xs2, xr2, gu, a_f, dgu_f, y32, ys, yr, st_s, st_r, dxin_s, dg_s,
     ld, wld, out_sem, st_sem, y_sem, sems,
 ):
     tok, hd, ff, qw = dims
@@ -87,21 +84,25 @@
         src, dst = ((wg_h, wg), (wu_h, wu))[i]
         return load(src.at[:, cols], dst.at[:, cols], wld.at[i, c])
 
+    def gu_load_start(c):
+        w_load(0, c).start()
+        w_load(1, c).start()
+
     for cp in small:
         cp.start()
     for i in range(qn):
         wq_load(i).start()
-    for c in range(nc):
-        w_load(0, c).start()
-        w_load(1, c).start()
-    for c in range(nc):
-        w_load(2, c).start()
 
     bar = pltpu.get_barrier_semaphore()
     for j in (1, 2, 3):
         pl.semaphore_signal(bar, inc=1, device_id=(zc, yc, lax.rem(h + j, 4)), device_id_type=MESH_ID)
     pl.semaphore_signal(bar, inc=1, device_id=ynb, device_id_type=MESH_ID)
-    pl.semaphore_wait(bar, 4)
+    small[0].wait()
+    gu_load_start(0)
+    x_f = x_s[...].astype(F32)
+    sq_part = jnp.sum(x_f * x_f, axis=-1, keepdims=True)
+    with jax.named_scope("barrier"):
+        pl.semaphore_wait(bar, 4)
 
     def stat_copy(n, j):
         return pltpu.make_async_remote_copy(
@@ -122,18 +123,21 @@
         return unpack_stats(st_r[n, 0] + st_r[n, 1] + st_r[n, 2] + st_r[n, 3], tok, count)
 
     def y_copy(n):
+        src, dst = (y32.at[0], y32.at[1]) if n == 0 else (ys.at[n - 1], yr.at[n - 1])
         return pltpu.make_async_remote_copy(
-            src_ref=ys.at[n], dst_ref=yr.at[n], send_sem=y_sem.at[n, 0], recv_sem=y_sem.at[n, 1],
+            src_ref=src, dst_ref=dst, send_sem=y_sem.at[n, 0], recv_sem=y_sem.at[n, 1],
             device_id=ynb, device_id_type=MESH_ID,
         )
 
     def y_sum(n):
-        y_copy(n).wait()
-        return ys[n].astype(F32) + yr[n].astype(F32)
-
-    small[0].wait()
-    x_f = x_s[...].astype(F32)
-    stat_send(0, [jnp.sum(x_f * x_f, axis=-1, keepdims=True)])
+        with jax.named_scope(f"ywait{n}"):
+            y_copy(n).wait()
+        if n == 0:
+            return y32[0] + y32[1]
+        return ys[n - 1].astype(F32) + yr[n - 1].astype(F32)
+
+    stat_send(0, [sq_part])
+    gu_load_start(1)
     small[2].wait()
     acc[...] = jnp.zeros_like(acc)
 
@@ -143,11 +147,14 @@
         acc[...] += nt_dot(dq[:, cols], wq[:, cols])
         return carry
 
-    lax.fori_loop(0, qn, qkv_step, 0)
-    ys[0] = acc[...].astype(BF)
+    with jax.named_scope("qkv"):
+        lax.fori_loop(0, qn, qkv_step, 0)
+    gu_load_start(2)
+    y32[0] = acc[...]
     y_copy(0).start()
     small[1].wait()
-    (sq,) = stat_recv(0, 1)
+    with jax.named_scope("stat0"):
+        (sq,) = stat_recv(0, 1)
     inv1 = lax.rsqrt(sq / d_model + NORM_EPS)
     n1[...] = (x_s[...].astype(F32) * inv1 * g1[...]).astype(BF)
     n1_out = load(n1, n1_o, out_sem.at[0])
@@ -190,7 +197,19 @@
     oth_cols = pl.ds(pl.multiple_of((1 - xc) * quart, quart), quart)
 
     def pipeline(ph, partial, activate, consume):
+        lag_pair, lag_act, lag_fwd, lag_dot = LAGS[ph]
+
         def step(t, carry):
+            if ph == 0:
+
+                @pl.when(t < nc - 3)
+                def _():
+                    gu_load_start(t + 3)
+
+                @pl.when((t >= 2) & (t < nc + 2))
+                def _():
+                    w_load(2, t - 2).start()
+
             @pl.when(t < nc)
             def _():
                 c = t
@@ -199,15 +218,17 @@
                 def _():
                     pair_copy(ph, c - 2).wait_send()
 
-                partial(c, 1 - core)
-                pair_copy(ph, c).start()
-                partial(c, core)
-
-            @pl.when((t >= LAG_PAIR) & (t < nc + LAG_PAIR))
+                with jax.named_scope(f"part{ph}"):
+                    partial(c, 1 - core)
+                    pair_copy(ph, c).start()
+                    partial(c, core)
+
+            @pl.when((t >= lag_pair) & (t < nc + lag_pair))
             def _():
-                c = t - LAG_PAIR
+                c = t - lag_pair
                 slot = lax.rem(c, 2)
-                pair_copy(ph, c).wait_recv()
+                with jax.named_scope(f"pairwait{ph}"):
+                    pair_copy(ph, c).wait_recv()
                 if ph == 0:
                     xs[c] = (part[slot, core, :, :, oth_cols] + r1[c, :, :, oth_cols]).astype(BF)
                     x_copy(ph, c).start()
@@ -217,26 +238,31 @@
                     x_copy(ph, c).start()
                     r2[c, :, own_cols] = part[slot, core, 0, :, own_cols] + r2[c, :, own_cols]
 
-            @pl.when((t >= LAG_ACT) & (t < nc + LAG_ACT))
+            @pl.when((t >= lag_act) & (t < nc + lag_act))
             def _():
-                c = t - LAG_ACT
-                x_copy(ph, c).wait_recv()
-                activate(c)
+                c = t - lag_act
+                with jax.named_scope(f"xwait{ph}"):
+                    x_copy(ph, c).wait_recv()
+                with jax.named_scope(f"act{ph}"):
+                    activate(c)
                 g_copy(ph, c, GX).start()
                 g_copy(ph, c, GP).start()
 
-            @pl.when((t >= LAG_FWD) & (t < nc + LAG_FWD))
+            @pl.when((t >= lag_fwd) & (t < nc + lag_fwd))
             def _():
-                c = t - LAG_FWD
-                g_copy(ph, c, GX).wait_recv()
+                c = t - lag_fwd
+                with jax.named_scope(f"gxwait{ph}"):
+                    g_copy(ph, c, GX).wait_recv()
                 g_copy(ph, c, FW).start()
 
-            @pl.when((t >= LAG_DOT) & (t < nc + LAG_DOT))
+            @pl.when((t >= lag_dot) & (t < nc + lag_dot))
             def _():
-                c = t - LAG_DOT
-                g_copy(ph, c, GP).wait_recv()
-                g_copy(ph, c, FW).wait_recv()
-                consume(c)
+                c = t - lag_dot
+                with jax.named_scope(f"gpwait{ph}"):
+                    g_copy(ph, c, GP).wait_recv()
+                    g_copy(ph, c, FW).wait_recv()
+                with jax.named_scope(f"dot{ph}"):
+                    consume(c)
                 x_copy(ph, c).wait_send()
                 g_copy(ph, c, GX).wait_send()
                 g_copy(ph, c, GP).wait_send()
@@ -244,7 +270,7 @@
 
             return carry
 
-        lax.fori_loop(0, nc + LAG_DOT, step, 0)
+        lax.fori_loop(0, nc + lag_dot, step, 0)
         pair_copy(ph, nc - 2).wait_send()
         pair_copy(ph, nc - 1).wait_send()
 
@@ -273,7 +299,7 @@
         acc[...] += nn_dot(a_f[:, rows], wd[rows, :])
 
     pipeline(0, gu_partial, act_forward, down_dot)
-    ys[1] = acc[...].astype(BF)
+    ys[0] = acc[...].astype(BF)
     y_copy(1).start()
     a_out = load(a_f, a_o, out_sem.at[1])
     a_out.start()
@@ -288,7 +314,8 @@
         jnp.sum(x2 * x2, axis=-1, keepdims=True),
         jnp.sum(g2[...] * acc[...] * x2, axis=-1, keepdims=True),
     ])
-    sq2, dot2 = stat_recv(1, 2)
+    with jax.named_scope("stat1"):
+        sq2, dot2 = stat_recv(1, 2)
     inv2 = lax.rsqrt(sq2 / d_model + NORM_EPS)
     x2 = x2_s[...].astype(F32)
     dz2 = inv2 * (g2[...] * acc[...]) - x2 * (inv2 * inv2 * inv2) * (dot2 / d_model)
@@ -321,13 +348,14 @@
     pipeline(1, da_partial, act_backward, dn1_dot)
     dgu_out = load(dgu_f, dgu_o, out_sem.at[4])
     dgu_out.start()
-    ys[2] = acc[...].astype(BF)
+    ys[1] = acc[...].astype(BF)
     y_copy(2).start()
 
     acc[...] = y_sum(2)
     stat_send(2, [jnp.sum(g1[...] * acc[...] * x_s[...].astype(F32), axis=-1, keepdims=True)])
     dg_s[1:2, :] = jnp.sum(acc[...] * x_s[...].astype(F32) * inv1, axis=0, keepdims=True)
-    (dot1,) = stat_recv(2, 1)
+    with jax.named_scope("stat2"):
+        (dot1,) = stat_recv(2, 1)
     dz1 = inv1 * (g1[...] * acc[...]) - x_s[...].astype(F32) * (inv1 * inv1 * inv1) * (dot1 / d_model)
     dxin_s[...] = (e_s[...] + dz1).astype(BF)
     tail = [
@@ -365,7 +393,7 @@
             vm(tok, hd, F32), vm(2, 2, 2, tok, half, F32), vm(nc, 2, tok, half, F32), vm(nc, tok, half, F32),
             vm(nc, 2, tok, quart, BF), vm(nc, 2, tok, quart, BF), vm(nc, tok, quart, BF), vm(nc, tok, quart, BF),
             vm(nc, 2, tok, quart, F32), vm(tok, ff, BF), vm(2, tok, ff, BF),
-            vm(3, tok, hd, BF), vm(3, tok, hd, BF), vm(3, 8, 128, F32), vm(3, 4, 8, 128, F32),
+            vm(2, tok, hd, F32), vm(2, tok, hd, BF), vm(2, tok, hd, BF), vm(3, 8, 128, F32), vm(3, 4, 8, 128, F32),
             vm(tok, hd, BF), vm(8, hd, F32),
             dma((5,)), dma((4, nc)), dma((8,)), dma((3, 2, 4)), dma((3, 2)), dma((2, 10, nc)),
         ],
@@ -380,9 +408,12 @@
 SLOTS = 3
 
 
-def grad_kernel(dims, n1, n2, eb, a_f, dgu, dq, dwg_o, dwu_o, dwd_o, dwq_o, n1_t, n2_t, bg, bu, bd, sem):
+def grad_kernel(dims, n1, n2, eb, a_f, dgu, dq, dx, dg1, dg2, dwg_o, dwu_o, dwd_o, dwq_o, dx_o, dg1_o, dg2_o, n1_t, n2_t, bg, bu, bd, sem):
     hd, ff, qw = dims
     nt, nq = ff // TILE, qw // TILE
+    dx_o[...] = dx[...]
+    dg1_o[...] = dg1[...]
+    dg2_o[...] = dg2[...]
     n1_t[...] = n1[...].astype(F32).T.astype(BF)
     n2_t[...] = n2[...].astype(F32).T.astype(BF)
 
@@ -442,15 +473,18 @@
         d_copy(i).wait()
 
 
-def grad_call(n1, n2, eb, a_full, dgu, d_qkv):
+def grad_call(n1, n2, eb, a_full, dgu, d_qkv, dx_in, dg1, dg2):
     tok, hd = n1.shape
     ff, qw = a_full.shape[1], d_qkv.shape[1]
     out = lambda *shape: jax.ShapeDtypeStruct(shape, BF)
     return pl.pallas_call(
         functools.partial(grad_kernel, (hd, ff, qw)),
-        out_shape=(out(hd, ff), out(hd, ff), out(ff, hd), out(hd, qw)),
-        in_specs=[pl.BlockSpec(memory_space=pltpu.VMEM)] * 6,
-        out_specs=[ANY] * 4,
+        out_shape=(
+            out(hd, ff), out(hd, ff), out(ff, hd), out(hd, qw),
+            out(tok, hd), jax.ShapeDtypeStruct((1, hd), F32), jax.ShapeDtypeStruct((1, hd), F32),
+        ),
+        in_specs=[pl.BlockSpec(memory_space=pltpu.VMEM)] * 9,
+        out_specs=[ANY] * 4 + [pl.BlockSpec(memory_space=pltpu.VMEM)] * 3,
         scratch_shapes=[
             pltpu.VMEM((hd, tok), BF), pltpu.VMEM((hd, tok), BF),
             pltpu.VMEM((SLOTS, hd, TILE), BF), pltpu.VMEM((SLOTS, hd, TILE), BF), pltpu.VMEM((SLOTS, TILE, hd), BF),
@@ -458,7 +492,7 @@
         ],
         compiler_params=pltpu.CompilerParams(vmem_limit_bytes=VMEM_LIMIT),
         name="weight_grads",
-    )(n1, n2, eb, a_full, dgu, d_qkv)
+    )(n1, n2, eb, a_full, dgu, d_qkv, dx_in, dg1, dg2)
 
 
 def solution(mesh):
@@ -467,7 +501,9 @@
         n1, n2, eb, a_full, dgu, dx_in, dg1, dg2 = comm_call(
             x_in, gain_one.reshape(1, hd), gain_two.reshape(1, hd), w_gate, w_up, w_down, w_qkv, dx_out, d_qkv
         )
-        dw_gate, dw_up, dw_down, dw_qkv = grad_call(n1, n2, eb, a_full, dgu, d_qkv)
+        dw_gate, dw_up, dw_down, dw_qkv, dx_in, dg1, dg2 = grad_call(
+            n1, n2, eb, a_full, dgu, d_qkv, dx_in, dg1, dg2
+        )
         return dx_in, dw_gate, dw_up, dw_down, dw_qkv, dg1.reshape(hd), dg2.reshape(hd)
 
     tok_spec = P("data", "hid")

time: 114 us -> 92 us (0.81)
  Pallas kernels: 109 us -> 91.3 us
  local copies, waits for them, and re-layouts: 4.11 us -> 0 us
    pallas_call x1, Pallas kernels: 87.7 us -> 69.1 us  [comm_call(): pl.pallas_call(functools.partial(comm_kernel, (tok, hd, ff, qw)), out_sha...]
    unnamed x3 -> x0, local copies, waits for them, and re-layouts: 4.11 us -> none
where the time goes in v2:
time: 92 us; the launch traced here: 91.9 us
  Pallas kernels  91.3 us (99%)
    pallas_call x1, Pallas kernels, comm_call(): pl.pallas_call(functools.partial(comm_kernel, (tok, hd, ff, qw)), out_sha...  69.1 us
    pallas_call x1, Pallas kernels, grad_call(): pl.pallas_call(functools.partial(grad_kernel, (hd, ff, qw)), out_shape=(o...  22.2 us

profile of v2, /device:TPU:0, one launch (start us, length us, event | category | flops | bytes accessed | tf_op | source)
XLA Modules:
  0.0 91.9 jit_solution(12447073027932654313)
XLA Ops:
  0.6 69.1 %block_comm.1 = (bf16[64,1024]{1,0:T(8,128)(2,1)}, bf16[64,1024]{1,0:T(8,128)(2,1)}, bf16[64,1024]{1,0:T(8,128)(2,1)}, bf16[64,7168]{1,0:T(8,128)(2,1)}, bf16[2,...) custom-call(bf16[64,1024]{1,0:T(8,128)(2,1)} %x_h.1, ...), custom_call_target="tpu_custom_call" | custom-call | tf_op jit(solution)/shard_map/block_comm/pallas_call | solution.py:381
  69.8 22.2 %weight_grads.1 = (bf16[1024,7168]{1,0:T(8,128)(2,1)}, bf16[1024,7168]{1,0:T(8,128)(2,1)}, bf16[7168,1024]{1,0:T(8,128)(2,1)}, bf16[1024,3072]{1,0:T(8,128)(2,1)...) custom-call(bf16[64,1024]{1,0:T(8,128)(2,1)} %get-tuple-element.22.n1, ...), custom_call_target="tpu_custom_call" | custom-call | tf_op jit(solution)/shard_map/weight_grads/pallas_call | solution.py:480

commit v3 on v2

v3 whole, which is shorter than its diff:
```python
import functools

import jax
import jax.numpy as jnp
from jax import lax
from jax.experimental import pallas as pl
from jax.experimental.pallas import tpu as pltpu
from jax.sharding import PartitionSpec as P

NORM_EPS = 1e-6
BF = jnp.bfloat16
F32 = jnp.float32
MESH_ID = pl.DeviceIdType.MESH
ANY = pl.BlockSpec(memory_space=pl.ANY)
VMEM_LIMIT = 67043328

CHUNK = 1024
LATE = 2
F_STEPS = (0, 3)
PIECES = (0, 1, 2, 4)
DIRECT_LAST = 1
DIRECT_FIRST = 1
LAGS = ((1, 3, 5, 6), (1, 3, 5, 6))

PAIR, XRED, GX, GP, FW, DG = range(6)

PEERS = tuple((dy, j) for dy in range(2) for j in range(4) if dy or j)
ROW_PEERS = PEERS[:3]


def nn_dot(a_mat, b_mat):
    return jnp.dot(a_mat, b_mat, preferred_element_type=F32)


def nt_dot(a_mat, b_mat):
    return lax.dot_general(a_mat, b_mat, (((1,), (1,)), ((), ())), preferred_element_type=F32)


def pack_stats(cols):
    tok = cols[0].shape[0]
    lane = lax.broadcasted_iota(jnp.int32, (tok, 128), 1)
    wide = jnp.zeros((tok, 128), F32)
    for i, col in enumerate(cols):
        wide = jnp.where(lane == i, col, wide)
    full = jnp.concatenate([wide, jnp.zeros((128 - tok, 128), F32)], axis=0)
    return full.T[0:8, :]


def unpack_stats(tile, tok, count):
    full = jnp.concatenate([tile, jnp.zeros((120, 128), F32)], axis=0).T
    return [full[0:tok, i : i + 1] for i in range(count)]


def comm_kernel(
    dims,
    x_h, g1_h, g2_h, wg_h, wu_h, wd_h, wq_h, dx_h, dq_h,
    n1_o, n2_o, eb_o, a_o, dgu_o, dxin_o, dg_o,
    wg, wu, wd, wq, dq, x_s, dx_s, g1, g2, n1, n2, eb, e_s, x2_s,
    acc, part, r1, r2, xs, xr, xs2, xr2, gu, fb, a_f, da_f, dgu_f, y32, ys, yr, st_s, st_r, dxin_s, dg_s,
    ld, wld, out_sem, st_sem, y_sem, recvs, sends, f_sem,
):
    tok, hd, ff, qw = dims
    c_w = CHUNK
    nc = ff // c_w
    half = c_w // 2
    quart = c_w // 4
    d_model = hd * 4
    zc, yc, h = lax.axis_index("data"), lax.axis_index("ffn"), lax.axis_index("hid")
    xc = h // 2
    core = lax.rem(h, 2)
    pair = (zc, yc, xc * 2 + 1 - core)
    xnb = (zc, yc, (1 - xc) * 2 + core)
    diag = (zc, yc, 3 - h)
    ynb = (zc, 1 - yc, h)

    def peer(dy, j):
        return (zc, lax.rem(yc + dy, 2), lax.rem(h + j, 4))


    def load(src, dst, sem):
        return pltpu.make_async_copy(src, dst, sem)

    small = [
        load(x_h, x_s, ld.at[0]), load(g1_h, g1, ld.at[1]), load(dq_h, dq, ld.at[2]),
        load(g2_h, g2, ld.at[3]), load(dx_h, dx_s, ld.at[4]),
    ]
    qn = qw // 1024

    def wq_load(i):
        cols = pl.ds(pl.multiple_of(i * 1024, 1024), 1024)
        return load(wq_h.at[:, cols], wq.at[:, cols], wld.at[2, i])

    pieces = [c for c in PIECES if c < nc]

    def gu_load(i, n):
        first = pieces[n]
        last = pieces[n + 1] if n + 1 < len(pieces) else nc
        cols = pl.ds(first * c_w, (last - first) * c_w)
        src, dst = ((wg_h, wg), (wu_h, wu))[i]
        return load(src.at[:, cols], dst.at[:, cols], wld.at[i, n])

    def gu_load_wait(c):
        for n, first in enumerate(pieces):

            @pl.when(c == first)
            def _():
                gu_load(0, n).wait()
                gu_load(1, n).wait()

    wd_load = load(wd_h, wd, ld.at[5])

    def gu_load_start(n):
        gu_load(0, n).start()
        gu_load(1, n).start()

    for cp in small:
        cp.start()
    for i in range(qn):
        wq_load(i).start()

    bar = pltpu.get_barrier_semaphore()
    for dy, j in PEERS[:4]:
        pl.semaphore_signal(bar, inc=1, device_id=peer(dy, j), device_id_type=MESH_ID)
    small[0].wait()
    gu_load_start(0)
    x_f = x_s[...].astype(F32)
    sq_part = jnp.sum(x_f * x_f, axis=-1, keepdims=True)

    def qkv_step(i, carry):
        wq_load(i).wait()
        cols = pl.ds(pl.multiple_of(i * 1024, 1024), 1024)
        y32[0] += nt_dot(dq[:, cols], wq[:, cols])
        return carry

    y32[0] = jnp.zeros((tok, hd), F32)
    with jax.named_scope("barrier"):
        pl.semaphore_wait(bar, 4)

    def stat_copy(n, i):
        return pltpu.make_async_remote_copy(
            src_ref=st_s.at[n], dst_ref=st_r.at[n, yc * 4 + h], send_sem=st_sem.at[n, 0], recv_sem=st_sem.at[n, 1],
            device_id=peer(*PEERS[i]), device_id_type=MESH_ID,
        )

    def stat_send(n, cols, peers=ROW_PEERS):
        tile = pack_stats(cols)
        st_s[n] = tile
        st_r[n, yc * 4 + h] = tile
        for i in range(len(peers)):
            stat_copy(n, i).start()

    def stat_recv(n, count, peers=ROW_PEERS):
        all_tiles = st_r.at[n, pl.ds(0, len(peers))]
        whole = pltpu.make_async_remote_copy(
            src_ref=all_tiles, dst_ref=all_tiles, send_sem=st_sem.at[n, 0], recv_sem=st_sem.at[n, 1],
            device_id=peer(*PEERS[0]), device_id_type=MESH_ID,
        )
        whole.wait()
        total = jnp.zeros((8, 128), F32)
        for i in range(len(peers) + 1):
            total += st_r[n, i] if peers is PEERS else st_r[n, yc * 4 + i]
        return unpack_stats(total, tok, count)

    def y_copy(n):
        src, dst = (y32.at[0], y32.at[1]) if n == 0 else (ys.at[n - 1], yr.at[n - 1])
        return pltpu.make_async_remote_copy(
            src_ref=src, dst_ref=dst, send_sem=y_sem.at[n, 0], recv_sem=y_sem.at[n, 1],
            device_id=ynb, device_id_type=MESH_ID,
        )

    def y_sum(n):
        with jax.named_scope(f"ywait{n}"):
            y_copy(n).wait()
        if n == 0:
            return y32[0] + y32[1]
        return ys[n - 1].astype(F32) + yr[n - 1].astype(F32)

    stat_send(0, [sq_part])
    gu_load_start(1)
    small[2].wait()
    with jax.named_scope("qkv"):
        lax.fori_loop(0, qn, qkv_step, 0)
    gu_load_start(2)
    y_copy(0).start()
    small[1].wait()
    with jax.named_scope("stat0"):
        (sq,) = stat_recv(0, 1)
    inv1 = lax.rsqrt(sq / d_model + NORM_EPS)
    n1[...] = (x_s[...].astype(F32) * inv1 * g1[...]).astype(BF)
    n1_out = load(n1, n1_o, out_sem.at[0])
    n1_out.start()
    acc[...] = jnp.zeros_like(acc)

    def pair_copy(ph, c):
        slot = lax.rem(c, 2)
        src = part.at[slot, 1 - core] if ph == 0 else part.at[slot, 1 - core, 0]
        return pltpu.make_async_remote_copy(
            src_ref=src, dst_ref=(r1 if ph == 0 else r2).at[c],
            send_sem=sends.at[4 + slot], recv_sem=recvs.at[PAIR, c],
            device_id=pair, device_id_type=MESH_ID,
        )

    def x_copy(ph, c):
        src, dst = ((xs, xr), (xs2, xr2))[ph]
        return pltpu.make_async_remote_copy(
            src_ref=src.at[c], dst_ref=dst.at[c],
            send_sem=sends.at[0], recv_sem=recvs.at[XRED, c],
            device_id=xnb, device_id_type=MESH_ID,
        )

    own_q = core * 2 + xc
    xnb_q = core * 2 + 1 - xc

    def block(ph, c, q):
        cols = pl.ds(pl.multiple_of(c * c_w + q * quart, quart), quart)
        return (a_f if ph == 0 else da_f).at[:, cols]

    def g_copy(ph, c, kind):
        ref = block(ph, c, xnb_q if kind == FW else own_q)
        target = {GX: xnb, GP: pair, FW: pair, DG: diag}[kind]
        kind = FW if kind == DG else kind
        return pltpu.make_async_remote_copy(
            src_ref=ref, dst_ref=ref, send_sem=sends.at[kind - 1], recv_sem=recvs.at[kind, c],
            device_id=target, device_id_type=MESH_ID,
        )

    def wait_sends(ph):
        src = xs if ph == 0 else xs2
        pltpu.make_async_remote_copy(
            src_ref=src, dst_ref=src, send_sem=sends.at[0], recv_sem=recvs.at[XRED, 0],
            device_id=xnb, device_id_type=MESH_ID,
        ).wait_send()
        whole = (a_f if ph == 0 else da_f).at[:, pl.ds(0, ff // 4)]
        for kind in (GX, GP, FW):
            pltpu.make_async_remote_copy(
                src_ref=whole, dst_ref=whole, send_sem=sends.at[kind - 1], recv_sem=recvs.at[kind, 0],
                device_id=xnb, device_id_type=MESH_ID,
            ).wait_send()
        for c in (nc - 2, nc - 1):
            pair_copy(ph, c).wait_send()

    f_parts = ((0, nc - LATE), (nc - LATE, LATE))

    def f_copy(n):
        first, count = f_parts[n % 2] if n < 4 else (0, nc)
        ref = fb.at[xnb_q if n in (2, 3) else own_q, pl.ds(first, count)]
        return pltpu.make_async_remote_copy(
            src_ref=ref, dst_ref=ref, send_sem=f_sem.at[n, 0], recv_sem=f_sem.at[n, 1],
            device_id=xnb if n < 2 else pair, device_id_type=MESH_ID,
        )

    own_cols = pl.ds(pl.multiple_of(xc * quart, quart), quart)
    oth_cols = pl.ds(pl.multiple_of((1 - xc) * quart, quart), quart)

    def pipeline(ph, partial, activate, consume):
        lag_pair, lag_act, lag_fwd, lag_dot = LAGS[ph]

        def direct(c):
            return c >= nc - DIRECT_LAST if ph == 0 else c < DIRECT_FIRST


        def step(t, carry):
            if ph == 1:
                for n, when in enumerate(F_STEPS):

                    @pl.when(t == when)
                    def _():
                        f_copy(n).wait_recv()
                        f_copy(2 + n).start()

            if ph == 0:

                @pl.when(t == 0)
                def _():
                    for n in range(3, len(pieces)):
                        gu_load_start(n)

                @pl.when(t == 2)
                def _():
                    wd_load.start()

            @pl.when(t < nc)
            def _():
                c = t

                @pl.when(c >= 2)
                def _():
                    pair_copy(ph, c - 2).wait_send()

                with jax.named_scope(f"part{ph}"):

                    @pl.when(c == 0)
                    def _():
                        partial(c, 1 - core)
                        pair_copy(ph, c).start()
                        partial(c, core)

                    @pl.when(c > 0)
                    def _():
                        partial(c, None)
                        pair_copy(ph, c).start()

            @pl.when((t >= lag_pair) & (t < nc + lag_pair))
            def _():
                c = t - lag_pair
                slot = lax.rem(c, 2)
                with jax.named_scope(f"pairwait{ph}"):
                    pair_copy(ph, c).wait_recv()
                if ph == 0:
                    xs[c] = (part[slot, core, :, :, oth_cols] + r1[c, :, :, oth_cols]).astype(BF)
                    x_copy(ph, c).start()
                    gu[c] = part[slot, core, :, :, own_cols] + r1[c, :, :, own_cols]
                else:
                    xs2[c] = (part[slot, core, 0, :, oth_cols] + r2[c, :, oth_cols]).astype(BF)
                    x_copy(ph, c).start()
                    r2[c, :, own_cols] = part[slot, core, 0, :, own_cols] + r2[c, :, own_cols]

            @pl.when((t >= lag_act) & (t < nc + lag_act))
            def _():
                c = t - lag_act
                with jax.named_scope(f"xwait{ph}"):
                    x_copy(ph, c).wait_recv()
                with jax.named_scope(f"act{ph}"):
                    activate(c)
                g_copy(ph, c, GX).start()
                g_copy(ph, c, GP).start()

                @pl.when(direct(c))
                def _():
                    g_copy(ph, c, DG).start()

                if ph == 0:

                    @pl.when(c == nc - 1)
                    def _():
                        f_copy(0).start()

            @pl.when((t >= lag_fwd) & (t < nc + lag_fwd))
            def _():
                c = t - lag_fwd
                with jax.named_scope(f"gxwait{ph}"):
                    g_copy(ph, c, GX).wait_recv()

                @pl.when(jnp.logical_not(direct(c)))
                def _():
                    g_copy(ph, c, FW).start()

            @pl.when((t >= lag_dot) & (t < nc + lag_dot))
            def _():
                c = t - lag_dot
                with jax.named_scope(f"gpwait{ph}"):
                    g_copy(ph, c, GP).wait_recv()
                    g_copy(ph, c, FW).wait_recv()
                with jax.named_scope(f"dot{ph}"):
                    consume(c)

            return carry

        lax.fori_loop(0, nc + lag_dot, step, 0)

    def gu_partial(c, which):
        if which is not core:
            gu_load_wait(c)
        slot = lax.rem(c, 2)
        for i, w in enumerate((wg, wu)):
            if which is None:
                prod = nn_dot(n1[...], w[:, pl.ds(pl.multiple_of(c * c_w, c_w), c_w)])
                part[slot, 0, i] = prod[:, :half]
                part[slot, 1, i] = prod[:, half:]
            else:
                part[slot, which, i] = nn_dot(n1[...], w[:, pl.ds(pl.multiple_of(c * c_w + which * half, half), half)])

    def act_forward(c):
        gate = gu[c, 0] + xr[c, 0].astype(F32)
        up = gu[c, 1] + xr[c, 1].astype(F32)
        sig = jax.nn.sigmoid(gate)
        silu = gate * sig
        cols = pl.ds(pl.multiple_of(c * c_w + own_q * quart, quart), quart)
        a_f[:, cols] = (silu * up).astype(BF)
        fb[own_q, c, 0] = (up * sig * (1.0 + gate * (1.0 - sig))).astype(BF)
        fb[own_q, c, 1] = silu.astype(BF)

    def down_dot(c):
        @pl.when(c == 0)
        def _():
            wd_load.wait()

        rows = pl.ds(pl.multiple_of(c * c_w, c_w), c_w)
        acc[...] += nn_dot(a_f[:, rows], wd[rows, :])

    pipeline(0, gu_partial, act_forward, down_dot)
    ys[0] = acc[...].astype(BF)
    y_copy(1).start()
    wait_sends(0)
    f_copy(4).start()
    a_out = load(a_f, a_o, out_sem.at[1])
    a_out.start()

    small[3].wait()
    small[4].wait()
    dn2 = y_sum(0)
    acc[...] = dn2
    x2_s[...] = (x_s[...].astype(F32) + y_sum(1)).astype(BF)
    x2 = x2_s[...].astype(F32)
    stat_send(1, [
        jnp.sum(x2 * x2, axis=-1, keepdims=True),
        jnp.sum(g2[...] * acc[...] * x2, axis=-1, keepdims=True),
    ])
    f_copy(1).start()
    with jax.named_scope("stat1"):
        sq2, dot2 = stat_recv(1, 2)
    inv2 = lax.rsqrt(sq2 / d_model + NORM_EPS)
    x2 = x2_s[...].astype(F32)
    dz2 = inv2 * (g2[...] * acc[...]) - x2 * (inv2 * inv2 * inv2) * (dot2 / d_model)
    e_val = dx_s[...].astype(F32) + dz2
    e_s[...] = e_val
    eb[...] = e_val.astype(BF)
    n2[...] = (x2_s[...].astype(F32) * inv2 * g2[...]).astype(BF)
    dg_s[0:1, :] = jnp.sum(acc[...] * x2_s[...].astype(F32) * inv2, axis=0, keepdims=True)
    outs = [load(eb, eb_o, out_sem.at[2]), load(n2, n2_o, out_sem.at[3])]
    for cp in outs:
        cp.start()
    acc[...] = jnp.zeros_like(acc)

    def da_partial(c, which):
        slot = lax.rem(c, 2)
        if which is None:
            prod = nt_dot(eb[...], wd[pl.ds(pl.multiple_of(c * c_w, c_w), c_w), :])
            part[slot, 0, 0] = prod[:, :half]
            part[slot, 1, 0] = prod[:, half:]
        else:
            part[slot, which, 0] = nt_dot(eb[...], wd[pl.ds(pl.multiple_of(c * c_w + which * half, half), half), :])

    def act_backward(c):
        cols = pl.ds(pl.multiple_of(c * c_w + own_q * quart, quart), quart)
        da_f[:, cols] = (r2[c, :, own_cols] + xr2[c].astype(F32)).astype(BF)

    def dn1_dot(c):
        @pl.when(c == 0)
        def _():
            f_copy(4).wait_recv()
            f_copy(2).wait_recv()

        @pl.when(c == nc - LATE)
        def _():
            f_copy(3).wait_recv()

        for q in range(4):
            cols = pl.ds(pl.multiple_of(c * c_w + q * quart, quart), quart)
            d_act = da_f[:, cols].astype(F32)
            for i in range(2):
                dgu_f[i, :, cols] = (d_act * fb[q, c, i].astype(F32)).astype(BF)
        cols = pl.ds(pl.multiple_of(c * c_w, c_w), c_w)
        acc[...] += nt_dot(dgu_f[0, :, cols], wg[:, cols]) + nt_dot(dgu_f[1, :, cols], wu[:, cols])
    pipeline(1, da_partial, act_backward, dn1_dot)
    dgu_out = load(dgu_f, dgu_o, out_sem.at[4])

    stat_send(2, [jnp.sum(g1[...] * acc[...] * x_s[...].astype(F32), axis=-1, keepdims=True)], PEERS)
    ys[1] = acc[...].astype(BF)
    y_copy(2).start()
    dgu_out.start()
    wait_sends(1)
    for n in range(5):
        f_copy(n).wait_send()
    acc[...] = y_sum(2)
    with jax.named_scope("fin0"):
      dg_s[1:2, :] = jnp.sum(acc[...] * x_s[...].astype(F32) * inv1, axis=0, keepdims=True)
    with jax.named_scope("stat2"):
        (dot1,) = stat_recv(2, 1, PEERS)
    with jax.named_scope("fin1"):
      dz1 = inv1 * (g1[...] * acc[...]) - x_s[...].astype(F32) * (inv1 * inv1 * inv1) * (dot1 / d_model)
      dxin_s[...] = (e_s[...] + dz1).astype(BF)
    tail = [
        load(dxin_s, dxin_o, out_sem.at[5]),
        load(dg_s, dg_o, out_sem.at[6]),
    ]
    for cp in tail:
        cp.start()
    with jax.named_scope("fin2"):
      for cp in (n1_out, a_out, *outs, dgu_out, *tail):
        cp.wait()


def comm_call(x_in, gain_one, gain_two, w_gate, w_up, w_down, w_qkv, dx_out, d_qkv):
    tok, hd = x_in.shape
    ff = w_gate.shape[1]
    qw = w_qkv.shape[1]
    nc = ff // CHUNK
    half, quart = CHUNK // 2, CHUNK // 4
    out = lambda shape, dtype: jax.ShapeDtypeStruct(shape, dtype)
    vm = lambda *shape_dtype: pltpu.VMEM(shape_dtype[:-1], shape_dtype[-1])
    dma = pltpu.SemaphoreType.DMA
    return pl.pallas_call(
        functools.partial(comm_kernel, (tok, hd, ff, qw)),
        out_shape=(
            out((tok, hd), BF), out((tok, hd), BF), out((tok, hd), BF), out((tok, ff), BF), out((2, tok, ff), BF),
            out((tok, hd), BF), out((8, hd), F32),
        ),
        in_specs=[ANY] * 9,
        out_specs=[ANY] * 7,
        scratch_shapes=[
            vm(hd, ff, BF), vm(hd, ff, BF), vm(ff, hd, BF), vm(hd, qw, BF), vm(tok, qw, BF),
            vm(tok, hd, BF), vm(tok, hd, BF), vm(1, hd, F32), vm(1, hd, F32),
            vm(tok, hd, BF), vm(tok, hd, BF), vm(tok, hd, BF), vm(tok, hd, F32), vm(tok, hd, BF),
            vm(tok, hd, F32), vm(2, 2, 2, tok, half, F32), vm(nc, 2, tok, half, F32), vm(nc, tok, half, F32),
            vm(nc, 2, tok, quart, BF), vm(nc, 2, tok, quart, BF), vm(nc, tok, quart, BF), vm(nc, tok, quart, BF),
            vm(nc, 2, tok, quart, F32), vm(4, nc, 2, tok, quart, BF), vm(tok, ff, BF), vm(tok, ff, BF), vm(2, tok, ff, BF),
            vm(2, tok, hd, F32), vm(2, tok, hd, BF), vm(2, tok, hd, BF), vm(3, 8, 128, F32), vm(3, 8, 8, 128, F32),
            vm(tok, hd, BF), vm(8, hd, F32),
            dma((6,)), dma((3, 4)), dma((7,)), dma((3, 2)), dma((3, 2)), dma((5, nc)), dma((6,)), dma((5, 2)),
        ],
        compiler_params=pltpu.CompilerParams(
            collective_id=0, has_side_effects=True, vmem_limit_bytes=VMEM_LIMIT
        ),
        name="block_comm",
    )(x_in, gain_one, gain_two, w_gate, w_up, w_down, w_qkv, dx_out, d_qkv)


TILE = 512
SLOTS = 3


def grad_kernel(
    dims, n1_h, n2_h, eb_h, a_h, dgu_h, dq_h, dx_h, dg_h,
    dwg_o, dwu_o, dwd_o, dwq_o, dx_o, dg1_o, dg2_o,
    n1, n2, eb, a_f, dgu, dq, dx, dg, n1_t, n2_t, bq, bg, bu, bd, ld, sem,
):
    hd, ff, qw = dims
    nt, nq = ff // TILE, qw // TILE
    pairs = ((n2_h, n2), (dq_h, dq), (eb_h, eb), (a_h, a_f), (n1_h, n1), (dgu_h, dgu), (dx_h, dx), (dg_h, dg))
    loads = [pltpu.make_async_copy(src, dst, ld.at[i]) for i, (src, dst) in enumerate(pairs)]
    for cp in loads:
        cp.start()

    def cols_of(i):
        return pl.ds(pl.multiple_of(i * TILE, TILE), TILE)

    def out_copy(kind, i):
        slot = lax.rem(i, SLOTS)
        src = (bq, bg, bu, bd)[kind].at[slot]
        dst = (dwq_o, dwg_o, dwu_o, dwd_o)[kind]
        return pltpu.make_async_copy(src, dst.at[cols_of(i), :] if kind == 3 else dst.at[:, cols_of(i)], sem.at[kind, slot])

    with jax.named_scope("b_in0"):
      loads[0].wait()
      loads[1].wait()
    with jax.named_scope("b_t"):
      n2_t[...] = n2[...].T

    def q_step(i, carry):
        @pl.when(i >= SLOTS)
        def _():
            out_copy(0, i - SLOTS).wait()

        bq[lax.rem(i, SLOTS)] = nn_dot(n2_t[...], dq[:, cols_of(i)]).astype(BF)
        out_copy(0, i).start()
        return carry

    with jax.named_scope("b_q"):
      lax.fori_loop(0, nq, q_step, 0)
    with jax.named_scope("b_in1"):
      for cp in loads[2:]:
        cp.wait()
    finals = [
        pltpu.make_async_copy(dx, dx_o, ld.at[0]),
        pltpu.make_async_copy(dg.at[0:1, :], dg2_o, ld.at[1]),
        pltpu.make_async_copy(dg.at[1:2, :], dg1_o, ld.at[2]),
    ]
    for cp in finals:
        cp.start()
    n1_t[...] = n1[...].T

    def step(i, carry):
        slot = lax.rem(i, SLOTS)

        with jax.named_scope("b_wait"):
          @pl.when(i >= SLOTS)
          def _():
            for kind in (1, 2, 3):
                out_copy(kind, i - SLOTS).wait()

        bd[slot] = nn_dot(a_f[:, cols_of(i)].T, eb[...]).astype(BF)
        out_copy(3, i).start()
        bg[slot] = nn_dot(n1_t[...], dgu[0, :, cols_of(i)]).astype(BF)
        out_copy(1, i).start()
        bu[slot] = nn_dot(n1_t[...], dgu[1, :, cols_of(i)]).astype(BF)
        out_copy(2, i).start()
        return carry

    lax.fori_loop(0, nt, step, 0)
    for cp in finals:
        cp.wait()
    with jax.named_scope("b_end"):
     for i in range(nq - SLOTS, nq):
        out_copy(0, i).wait()
     for i in range(nt - SLOTS, nt):
        for kind in (1, 2, 3):
            out_copy(kind, i).wait()


def grad_call(n1, n2, eb, a_full, dgu, d_qkv, dx_in, dg):
    tok, hd = n1.shape
    ff, qw = a_full.shape[1], d_qkv.shape[1]
    out = lambda *shape: jax.ShapeDtypeStruct(shape, BF)
    vm = lambda *shape: pltpu.VMEM(shape, BF)
    return pl.pallas_call(
        functools.partial(grad_kernel, (hd, ff, qw)),
        out_shape=(
            out(hd, ff), out(hd, ff), out(ff, hd), out(hd, qw),
            out(tok, hd), jax.ShapeDtypeStruct((1, hd), F32), jax.ShapeDtypeStruct((1, hd), F32),
        ),
        in_specs=[ANY] * 8,
        out_specs=[ANY] * 7,
        scratch_shapes=[
            vm(tok, hd), vm(tok, hd), vm(tok, hd), vm(tok, ff), vm(2, tok, ff), vm(tok, qw), vm(tok, hd), pltpu.VMEM((8, hd), F32), vm(hd, tok), vm(hd, tok),
            vm(SLOTS, hd, TILE), vm(SLOTS, hd, TILE), vm(SLOTS, hd, TILE), vm(SLOTS, TILE, hd),
            pltpu.SemaphoreType.DMA((8,)), pltpu.SemaphoreType.DMA((4, SLOTS)),
        ],
        compiler_params=pltpu.CompilerParams(vmem_limit_bytes=VMEM_LIMIT),
        name="weight_grads",
    )(n1, n2, eb, a_full, dgu, d_qkv, dx_in, dg)


def solution(mesh):
    def local_step(x_in, gain_one, gain_two, w_gate, w_up, w_down, w_qkv, dx_out, d_qkv):
        hd = x_in.shape[1]
        n1, n2, eb, a_full, dgu, dx_in, dg = comm_call(
            x_in, gain_one.reshape(1, hd), gain_two.reshape(1, hd), w_gate, w_up, w_down, w_qkv, dx_out, d_qkv
        )
        dw_gate, dw_up, dw_down, dw_qkv, dx_in, dg1, dg2 = grad_call(
            n1, n2, eb, a_full, dgu, d_qkv, dx_in, dg
        )
        return dx_in, dw_gate, dw_up, dw_down, dw_qkv, dg1.reshape(hd), dg2.reshape(hd)

    tok_spec = P("data", "hid")
    in_specs = (tok_spec, P("hid"), P("hid"), P("hid", "ffn"), P("hid", "ffn"), P("ffn", "hid"), P("hid", "ffn"), tok_spec, P("data", "ffn"))
    out_specs = (tok_spec, P(("data", "hid"), "ffn"), P(("data", "hid"), "ffn"), P(("data", "ffn"), "hid"), P(("data", "hid"), "ffn"), P(("data", "hid")), P(("data", "hid")))
    return jax.shard_map(local_step, mesh=mesh, in_specs=in_specs, out_specs=out_specs, check_vma=False)
```

time: 92 us -> 84.4 us (0.917)
  Pallas kernels: 91.3 us -> 83.6 us
    pallas_call x1, Pallas kernels: 69.1 us -> 64.3 us  [comm_call(): pl.pallas_call(functools.partial(comm_kernel, (tok, hd, ff, qw)), out_sha...]
    pallas_call x1, Pallas kernels: 22.2 us -> 19.3 us  [grad_call(): pl.pallas_call(functools.partial(grad_kernel, (hd, ff, qw)), out_shape=(o...]
where the time goes in v3:
time: 84.4 us; the launch traced here: 84.3 us
  Pallas kernels  83.6 us (99%)
    pallas_call x1, Pallas kernels, comm_call(): pl.pallas_call(functools.partial(comm_kernel, (tok, hd, ff, qw)), out_sha...  64.3 us
    pallas_call x1, Pallas kernels, grad_call(): pl.pallas_call(functools.partial(grad_kernel, (hd, ff, qw)), out_shape=(o...  19.3 us

profile of v3, /device:TPU:0, one launch (start us, length us, event | category | flops | bytes accessed | tf_op | source)
XLA Modules:
  0.0 84.3 jit_solution(7439475458150196183)
XLA Ops:
  0.6 64.3 %block_comm.1 = (bf16[64,1024]{1,0:T(8,128)(2,1)}, bf16[64,1024]{1,0:T(8,128)(2,1)}, bf16[64,1024]{1,0:T(8,128)(2,1)}, bf16[64,7168]{1,0:T(8,128)(2,1)}, bf16[2,...) custom-call(bf16[64,1024]{1,0:T(8,128)(2,1)} %x_h.1, f32[1,1024]{1,0:T(1,128)} %bitcast.4, ...), custom_call_target="tpu_custom_call" | custom-call | tf_op jit(solution)/shard_map/block_comm/pallas_call | solution.py:493
  64.9 19.3 %weight_grads.1 = (bf16[1024,7168]{1,0:T(8,128)(2,1)}, bf16[1024,7168]{1,0:T(8,128)(2,1)}, bf16[7168,1024]{1,0:T(8,128)(2,1)}, bf16[1024,3072]{1,0:T(8,128)(2,1)...) custom-call(bf16[64,1024]{1,0:T(8,128)(2,1)} %get-tuple-element.21.n1_h, ...), custom_call_target="tpu_custom_call" | custom-call | tf_op jit(solution)/shard_map/weight_grads/pallas_call | solution.py:606

commit v4 on v3

--- a/solution.py
+++ b/solution.py
@@ -16,11 +16,12 @@
 
 CHUNK = 1024
 LATE = 2
+YB = 2
 F_STEPS = (0, 3)
-PIECES = (0, 1, 2, 4)
+QKV_AT = 7
 DIRECT_LAST = 1
-DIRECT_FIRST = 1
-LAGS = ((1, 3, 5, 6), (1, 3, 5, 6))
+DIRECT_FIRST = 0
+LAGS = ((1, 4, 7, 8), (1, 3, 5, 6))
 
 PAIR, XRED, GX, GP, FW, DG = range(6)
 
@@ -55,9 +56,9 @@
     dims,
     x_h, g1_h, g2_h, wg_h, wu_h, wd_h, wq_h, dx_h, dq_h,
     n1_o, n2_o, eb_o, a_o, dgu_o, dxin_o, dg_o,
-    wg, wu, wd, wq, dq, x_s, dx_s, g1, g2, n1, n2, eb, e_s, x2_s,
+    wgu, wd, wq, dq, x_s, dx_s, g1, g2, n1, n2, eb, e_s, x2_s,
     acc, part, r1, r2, xs, xr, xs2, xr2, gu, fb, a_f, da_f, dgu_f, y32, ys, yr, st_s, st_r, dxin_s, dg_s,
-    ld, wld, out_sem, st_sem, y_sem, recvs, sends, f_sem,
+    ld, wld, qld, out_sem, st_sem, y_sem, recvs, sends, f_sem,
 ):
     tok, hd, ff, qw = dims
     c_w = CHUNK
@@ -88,24 +89,12 @@
 
     def wq_load(i):
         cols = pl.ds(pl.multiple_of(i * 1024, 1024), 1024)
-        return load(wq_h.at[:, cols], wq.at[:, cols], wld.at[2, i])
-
-    pieces = [c for c in PIECES if c < nc]
-
-    def gu_load(i, n):
-        first = pieces[n]
-        last = pieces[n + 1] if n + 1 < len(pieces) else nc
-        cols = pl.ds(first * c_w, (last - first) * c_w)
-        src, dst = ((wg_h, wg), (wu_h, wu))[i]
-        return load(src.at[:, cols], dst.at[:, cols], wld.at[i, n])
-
-    def gu_load_wait(c):
-        for n, first in enumerate(pieces):
-
-            @pl.when(c == first)
-            def _():
-                gu_load(0, n).wait()
-                gu_load(1, n).wait()
+        return load(wq_h.at[:, cols], wq.at[:, cols], qld.at[i])
+
+    def gu_load(i, c):
+        src = (wg_h, wu_h)[i].at[:, pl.ds(pl.multiple_of(c * c_w, c_w), c_w)]
+        dst = wgu.at[:, pl.ds(pl.multiple_of((2 * c + i) * c_w, c_w), c_w)]
+        return load(src, dst, wld.at[i, c])
 
     wd_load = load(wd_h, wd, ld.at[5])
 
@@ -115,22 +104,20 @@
 
     for cp in small:
         cp.start()
-    for i in range(qn):
-        wq_load(i).start()
 
     bar = pltpu.get_barrier_semaphore()
     for dy, j in PEERS[:4]:
         pl.semaphore_signal(bar, inc=1, device_id=peer(dy, j), device_id_type=MESH_ID)
     small[0].wait()
     gu_load_start(0)
+    gu_load_start(1)
     x_f = x_s[...].astype(F32)
     sq_part = jnp.sum(x_f * x_f, axis=-1, keepdims=True)
 
-    def qkv_step(i, carry):
+    def qkv_step(i):
         wq_load(i).wait()
         cols = pl.ds(pl.multiple_of(i * 1024, 1024), 1024)
         y32[0] += nt_dot(dq[:, cols], wq[:, cols])
-        return carry
 
     y32[0] = jnp.zeros((tok, hd), F32)
     with jax.named_scope("barrier"):
@@ -161,30 +148,46 @@
             total += st_r[n, i] if peers is PEERS else st_r[n, yc * 4 + i]
         return unpack_stats(total, tok, count)
 
-    def y_copy(n):
-        src, dst = (y32.at[0], y32.at[1]) if n == 0 else (ys.at[n - 1], yr.at[n - 1])
+    yb = hd // YB
+
+    def y_cols(j):
+        return pl.ds(j * yb, yb)
+
+    def y_copy(n, j=0):
+        if n == 0:
+            src, dst = y32.at[0], y32.at[1]
+        else:
+            src, dst = ys.at[n - 1, :, y_cols(j)], yr.at[n - 1, :, y_cols(j)]
         return pltpu.make_async_remote_copy(
-            src_ref=src, dst_ref=dst, send_sem=y_sem.at[n, 0], recv_sem=y_sem.at[n, 1],
+            src_ref=src, dst_ref=dst, send_sem=y_sem.at[n, YB], recv_sem=y_sem.at[n, j],
             device_id=ynb, device_id_type=MESH_ID,
         )
 
-    def y_sum(n):
+    def y_send(n, j):
+        ys[n - 1, :, y_cols(j)] = acc[:, y_cols(j)].astype(BF)
+        y_copy(n, j).start()
+
+    def y_sum(n, j):
         with jax.named_scope(f"ywait{n}"):
-            y_copy(n).wait()
-        if n == 0:
-            return y32[0] + y32[1]
-        return ys[n - 1].astype(F32) + yr[n - 1].astype(F32)
+            y_copy(n, j).wait_recv()
+        return ys[n - 1, :, y_cols(j)].astype(F32) + yr[n - 1, :, y_cols(j)].astype(F32)
+
+    def y_wait_send(n):
+        whole = ys.at[n - 1]
+        pltpu.make_async_remote_copy(
+            src_ref=whole, dst_ref=whole, send_sem=y_sem.at[n, YB], recv_sem=y_sem.at[n, 0],
+            device_id=ynb, device_id_type=MESH_ID,
+        ).wait_send()
 
     stat_send(0, [sq_part])
-    gu_load_start(1)
+    gu_load_start(2)
+    gu_load_start(3)
     small[2].wait()
-    with jax.named_scope("qkv"):
-        lax.fori_loop(0, qn, qkv_step, 0)
-    gu_load_start(2)
-    y_copy(0).start()
     small[1].wait()
     with jax.named_scope("stat0"):
         (sq,) = stat_recv(0, 1)
+    gu_load_start(4)
+    gu_load_start(5)
     inv1 = lax.rsqrt(sq / d_model + NORM_EPS)
     n1[...] = (x_s[...].astype(F32) * inv1 * g1[...]).astype(BF)
     n1_out = load(n1, n1_o, out_sem.at[0])
@@ -259,6 +262,19 @@
             return c >= nc - DIRECT_LAST if ph == 0 else c < DIRECT_FIRST
 
 
+        def reduce_pair(c):
+            slot = lax.rem(c, 2)
+            with jax.named_scope(f"pairwait{ph}"):
+                pair_copy(ph, c).wait_recv()
+            if ph == 0:
+                xs[c] = (part[slot, core, :, :, oth_cols] + r1[c, :, :, oth_cols]).astype(BF)
+                x_copy(ph, c).start()
+                gu[c] = part[slot, core, :, :, own_cols] + r1[c, :, :, own_cols]
+            else:
+                xs2[c] = (part[slot, core, 0, :, oth_cols] + r2[c, :, oth_cols]).astype(BF)
+                x_copy(ph, c).start()
+                r2[c, :, own_cols] = part[slot, core, 0, :, own_cols] + r2[c, :, own_cols]
+
         def step(t, carry):
             if ph == 1:
                 for n, when in enumerate(F_STEPS):
@@ -272,12 +288,26 @@
 
                 @pl.when(t == 0)
                 def _():
-                    for n in range(3, len(pieces)):
-                        gu_load_start(n)
+                    for c in range(6, nc):
+                        gu_load_start(c)
+
+                @pl.when(t == 1)
+                def _():
+                    for i in range(qn):
+                        wq_load(i).start()
 
                 @pl.when(t == 2)
                 def _():
                     wd_load.start()
+
+                @pl.when((t >= QKV_AT) & (t < QKV_AT + qn))
+                def _():
+                    with jax.named_scope("qkv"):
+                        qkv_step(t - QKV_AT)
+
+                @pl.when(t == QKV_AT + qn - 1)
+                def _():
+                    y_copy(0).start()
 
             @pl.when(t < nc)
             def _():
@@ -294,26 +324,16 @@
                         partial(c, 1 - core)
                         pair_copy(ph, c).start()
                         partial(c, core)
+                        reduce_pair(c)
 
                     @pl.when(c > 0)
                     def _():
                         partial(c, None)
                         pair_copy(ph, c).start()
 
-            @pl.when((t >= lag_pair) & (t < nc + lag_pair))
+            @pl.when((t > lag_pair) & (t < nc + lag_pair))
             def _():
-                c = t - lag_pair
-                slot = lax.rem(c, 2)
-                with jax.named_scope(f"pairwait{ph}"):
-                    pair_copy(ph, c).wait_recv()
-                if ph == 0:
-                    xs[c] = (part[slot, core, :, :, oth_cols] + r1[c, :, :, oth_cols]).astype(BF)
-                    x_copy(ph, c).start()
-                    gu[c] = part[slot, core, :, :, own_cols] + r1[c, :, :, own_cols]
-                else:
-                    xs2[c] = (part[slot, core, 0, :, oth_cols] + r2[c, :, oth_cols]).astype(BF)
-                    x_copy(ph, c).start()
-                    r2[c, :, own_cols] = part[slot, core, 0, :, own_cols] + r2[c, :, own_cols]
+                reduce_pair(t - lag_pair)
 
             @pl.when((t >= lag_act) & (t < nc + lag_act))
             def _():
@@ -360,15 +380,18 @@
 
     def gu_partial(c, which):
         if which is not core:
-            gu_load_wait(c)
+            gu_load(0, c).wait()
+            gu_load(1, c).wait()
         slot = lax.rem(c, 2)
-        for i, w in enumerate((wg, wu)):
-            if which is None:
-                prod = nn_dot(n1[...], w[:, pl.ds(pl.multiple_of(c * c_w, c_w), c_w)])
-                part[slot, 0, i] = prod[:, :half]
-                part[slot, 1, i] = prod[:, half:]
-            else:
-                part[slot, which, i] = nn_dot(n1[...], w[:, pl.ds(pl.multiple_of(c * c_w + which * half, half), half)])
+        if which is None:
+            prod = nn_dot(n1[...], wgu[:, pl.ds(pl.multiple_of(2 * c * c_w, 2 * c_w), 2 * c_w)])
+            for i in range(2):
+                part[slot, 0, i] = prod[:, i * c_w : i * c_w + half]
+                part[slot, 1, i] = prod[:, i * c_w + half : (i + 1) * c_w]
+        else:
+            for i in range(2):
+                cols = pl.ds(pl.multiple_of((2 * c + i) * c_w + which * half, half), half)
+                part[slot, which, i] = nn_dot(n1[...], wgu[:, cols])
 
     def act_forward(c):
         gate = gu[c, 0] + xr[c, 0].astype(F32)
@@ -386,11 +409,19 @@
             wd_load.wait()
 
         rows = pl.ds(pl.multiple_of(c * c_w, c_w), c_w)
-        acc[...] += nn_dot(a_f[:, rows], wd[rows, :])
+
+        @pl.when(c < nc - 1)
+        def _():
+            acc[...] += nn_dot(a_f[:, rows], wd[rows, :])
+
+        @pl.when(c == nc - 1)
+        def _():
+            for j in range(YB):
+                acc[:, y_cols(j)] += nn_dot(a_f[:, rows], wd[rows, y_cols(j)])
+                y_send(1, j)
+
 
     pipeline(0, gu_partial, act_forward, down_dot)
-    ys[0] = acc[...].astype(BF)
-    y_copy(1).start()
     wait_sends(0)
     f_copy(4).start()
     a_out = load(a_f, a_o, out_sem.at[1])
@@ -398,14 +429,18 @@
 
     small[3].wait()
     small[4].wait()
-    dn2 = y_sum(0)
-    acc[...] = dn2
-    x2_s[...] = (x_s[...].astype(F32) + y_sum(1)).astype(BF)
-    x2 = x2_s[...].astype(F32)
-    stat_send(1, [
-        jnp.sum(x2 * x2, axis=-1, keepdims=True),
-        jnp.sum(g2[...] * acc[...] * x2, axis=-1, keepdims=True),
-    ])
+    y_copy(0).wait()
+    acc[...] = y32[0] + y32[1]
+    sq_two = jnp.zeros((tok, 1), F32)
+    dot_two = jnp.zeros((tok, 1), F32)
+    for j in range(YB):
+        cols = y_cols(j)
+        x2_b = (x_s[:, cols].astype(F32) + y_sum(1, j)).astype(BF)
+        x2_s[:, cols] = x2_b
+        x2 = x2_b.astype(F32)
+        sq_two += jnp.sum(x2 * x2, axis=-1, keepdims=True)
+        dot_two += jnp.sum(g2[:, cols] * acc[:, cols] * x2, axis=-1, keepdims=True)
+    stat_send(1, [sq_two, dot_two])
     f_copy(1).start()
     with jax.named_scope("stat1"):
         sq2, dot2 = stat_recv(1, 2)
@@ -449,20 +484,32 @@
             cols = pl.ds(pl.multiple_of(c * c_w + q * quart, quart), quart)
             d_act = da_f[:, cols].astype(F32)
             for i in range(2):
-                dgu_f[i, :, cols] = (d_act * fb[q, c, i].astype(F32)).astype(BF)
-        cols = pl.ds(pl.multiple_of(c * c_w, c_w), c_w)
-        acc[...] += nt_dot(dgu_f[0, :, cols], wg[:, cols]) + nt_dot(dgu_f[1, :, cols], wu[:, cols])
+                dst = pl.ds(pl.multiple_of((2 * c + i) * c_w + q * quart, quart), quart)
+                dgu_f[:, dst] = (d_act * fb[q, c, i].astype(F32)).astype(BF)
+        cols = pl.ds(pl.multiple_of(2 * c * c_w, 2 * c_w), 2 * c_w)
+
+        @pl.when(c < nc - 1)
+        def _():
+            acc[...] += nt_dot(dgu_f[:, cols], wgu[:, cols])
+
+        @pl.when(c == nc - 1)
+        def _():
+            for j in range(YB):
+                acc[:, y_cols(j)] += nt_dot(dgu_f[:, cols], wgu[y_cols(j), cols])
+                y_send(2, j)
+
     pipeline(1, da_partial, act_backward, dn1_dot)
     dgu_out = load(dgu_f, dgu_o, out_sem.at[4])
 
     stat_send(2, [jnp.sum(g1[...] * acc[...] * x_s[...].astype(F32), axis=-1, keepdims=True)], PEERS)
-    ys[1] = acc[...].astype(BF)
-    y_copy(2).start()
     dgu_out.start()
     wait_sends(1)
     for n in range(5):
         f_copy(n).wait_send()
-    acc[...] = y_sum(2)
+    for j in range(YB):
+        acc[:, y_cols(j)] = y_sum(2, j)
+    y_wait_send(1)
+    y_wait_send(2)
     with jax.named_scope("fin0"):
       dg_s[1:2, :] = jnp.sum(acc[...] * x_s[...].astype(F32) * inv1, axis=0, keepdims=True)
     with jax.named_scope("stat2"):
@@ -493,21 +540,21 @@
     return pl.pallas_call(
         functools.partial(comm_kernel, (tok, hd, ff, qw)),
         out_shape=(
-            out((tok, hd), BF), out((tok, hd), BF), out((tok, hd), BF), out((tok, ff), BF), out((2, tok, ff), BF),
+            out((tok, hd), BF), out((tok, hd), BF), out((tok, hd), BF), out((tok, ff), BF), out((tok, 2 * ff), BF),
             out((tok, hd), BF), out((8, hd), F32),
         ),
         in_specs=[ANY] * 9,
         out_specs=[ANY] * 7,
         scratch_shapes=[
-            vm(hd, ff, BF), vm(hd, ff, BF), vm(ff, hd, BF), vm(hd, qw, BF), vm(tok, qw, BF),
+            vm(hd, 2 * ff, BF), vm(ff, hd, BF), vm(hd, qw, BF), vm(tok, qw, BF),
             vm(tok, hd, BF), vm(tok, hd, BF), vm(1, hd, F32), vm(1, hd, F32),
             vm(tok, hd, BF), vm(tok, hd, BF), vm(tok, hd, BF), vm(tok, hd, F32), vm(tok, hd, BF),
             vm(tok, hd, F32), vm(2, 2, 2, tok, half, F32), vm(nc, 2, tok, half, F32), vm(nc, tok, half, F32),
             vm(nc, 2, tok, quart, BF), vm(nc, 2, tok, quart, BF), vm(nc, tok, quart, BF), vm(nc, tok, quart, BF),
-            vm(nc, 2, tok, quart, F32), vm(4, nc, 2, tok, quart, BF), vm(tok, ff, BF), vm(tok, ff, BF), vm(2, tok, ff, BF),
+            vm(nc, 2, tok, quart, F32), vm(4, nc, 2, tok, quart, BF), vm(tok, ff, BF), vm(tok, ff, BF), vm(tok, 2 * ff, BF),
             vm(2, tok, hd, F32), vm(2, tok, hd, BF), vm(2, tok, hd, BF), vm(3, 8, 128, F32), vm(3, 8, 8, 128, F32),
             vm(tok, hd, BF), vm(8, hd, F32),
-            dma((6,)), dma((3, 4)), dma((7,)), dma((3, 2)), dma((3, 2)), dma((5, nc)), dma((6,)), dma((5, 2)),
+            dma((6,)), dma((2, nc)), dma((qw // 1024,)), dma((7,)), dma((3, 2)), dma((3, YB + 1)), dma((5, nc)), dma((6,)), dma((5, 2)),
         ],
         compiler_params=pltpu.CompilerParams(
             collective_id=0, has_side_effects=True, vmem_limit_bytes=VMEM_LIMIT
@@ -516,8 +563,8 @@
     )(x_in, gain_one, gain_two, w_gate, w_up, w_down, w_qkv, dx_out, d_qkv)
 
 
-TILE = 512
-SLOTS = 3
+TILE = CHUNK
+SLOTS = 2
 
 
 def grad_kernel(
@@ -581,9 +628,9 @@
 
         bd[slot] = nn_dot(a_f[:, cols_of(i)].T, eb[...]).astype(BF)
         out_copy(3, i).start()
-        bg[slot] = nn_dot(n1_t[...], dgu[0, :, cols_of(i)]).astype(BF)
+        bg[slot] = nn_dot(n1_t[...], dgu[:, cols_of(2 * i)]).astype(BF)
         out_copy(1, i).start()
-        bu[slot] = nn_dot(n1_t[...], dgu[1, :, cols_of(i)]).astype(BF)
+        bu[slot] = nn_dot(n1_t[...], dgu[:, cols_of(2 * i + 1)]).astype(BF)
         out_copy(2, i).start()
         return carry
 
@@ -612,7 +659,7 @@
         in_specs=[ANY] * 8,
         out_specs=[ANY] * 7,
         scratch_shapes=[
-            vm(tok, hd), vm(tok, hd), vm(tok, hd), vm(tok, ff), vm(2, tok, ff), vm(tok, qw), vm(tok, hd), pltpu.VMEM((8, hd), F32), vm(hd, tok), vm(hd, tok),
+            vm(tok, hd), vm(tok, hd), vm(tok, hd), vm(tok, ff), vm(tok, 2 * ff), vm(tok, qw), vm(tok, hd), pltpu.VMEM((8, hd), F32), vm(hd, tok), vm(hd, tok),
             vm(SLOTS, hd, TILE), vm(SLOTS, hd, TILE), vm(SLOTS, hd, TILE), vm(SLOTS, TILE, hd),
             pltpu.SemaphoreType.DMA((8,)), pltpu.SemaphoreType.DMA((4, SLOTS)),
         ],

time: 84.4 us -> 81.9 us (0.970)
  Pallas kernels: 83.6 us -> 81.1 us
    pallas_call x1, Pallas kernels: 64.3 us -> 62.3 us  [comm_call(): pl.pallas_call(functools.partial(comm_kernel, (tok, hd, ff, qw)), out_sha...]
where the time goes in v4:
time: 81.9 us; the launch traced here: 81.7 us
  Pallas kernels  81.1 us (99%)
    pallas_call x1, Pallas kernels, comm_call(): pl.pallas_call(functools.partial(comm_kernel, (tok, hd, ff, qw)), out_sha...  62.3 us
    pallas_call x1, Pallas kernels, grad_call(): pl.pallas_call(functools.partial(grad_kernel, (hd, ff, qw)), out_shape=(o...  18.8 us

profile of v4, /device:TPU:0, one launch (start us, length us, event | category | flops | bytes accessed | tf_op | source)
XLA Modules:
  0.0 81.7 jit_solution(12293331963199760873)
XLA Ops:
  0.6 62.3 %block_comm.1 = (bf16[64,1024]{1,0:T(8,128)(2,1)}, bf16[64,1024]{1,0:T(8,128)(2,1)}, bf16[64,1024]{1,0:T(8,128)(2,1)}, bf16[64,7168]{1,0:T(8,128)(2,1)}, bf16[64...) custom-call(bf16[64,1024]{1,0:T(8,128)(2,1)} %x_h.1, f32[1,1024]{1,0:T(1,128)} %bitcast.4, ...), custom_call_target="tpu_custom_call" | custom-call | tf_op jit(solution)/shard_map/block_comm/pallas_call | solution.py:540
  62.9 18.8 %weight_grads.1 = (bf16[1024,7168]{1,0:T(8,128)(2,1)}, bf16[1024,7168]{1,0:T(8,128)(2,1)}, bf16[7168,1024]{1,0:T(8,128)(2,1)}, bf16[1024,3072]{1,0:T(8,128)(2,1)...) custom-call(bf16[64,1024]{1,0:T(8,128)(2,1)} %get-tuple-element.21.n1_h, ...), custom_call_target="tpu_custom_call" | custom-call | tf_op jit(solution)/shard_map/weight_grads/pallas_call | solution.py:653

commit v5 on v4

--- a/solution.py
+++ b/solution.py
@@ -21,7 +21,7 @@
 QKV_AT = 7
 DIRECT_LAST = 1
 DIRECT_FIRST = 0
-LAGS = ((1, 4, 7, 8), (1, 3, 5, 6))
+LAGS = ((1, 5, 9, 10), (1, 3, 5, 6))
 
 PAIR, XRED, GX, GP, FW, DG = range(6)
 
@@ -58,7 +58,7 @@
     n1_o, n2_o, eb_o, a_o, dgu_o, dxin_o, dg_o,
     wgu, wd, wq, dq, x_s, dx_s, g1, g2, n1, n2, eb, e_s, x2_s,
     acc, part, r1, r2, xs, xr, xs2, xr2, gu, fb, a_f, da_f, dgu_f, y32, ys, yr, st_s, st_r, dxin_s, dg_s,
-    ld, wld, qld, out_sem, st_sem, y_sem, recvs, sends, f_sem,
+    ld, wld, qld, st_sem, y_sem, recvs, sends, f_sem,
 ):
     tok, hd, ff, qw = dims
     c_w = CHUNK
@@ -87,14 +87,16 @@
     ]
     qn = qw // 1024
 
-    def wq_load(i):
-        cols = pl.ds(pl.multiple_of(i * 1024, 1024), 1024)
-        return load(wq_h.at[:, cols], wq.at[:, cols], qld.at[i])
+    wq_load = load(wq_h, wq, qld.at[0])
 
     def gu_load(i, c):
         src = (wg_h, wu_h)[i].at[:, pl.ds(pl.multiple_of(c * c_w, c_w), c_w)]
         dst = wgu.at[:, pl.ds(pl.multiple_of((2 * c + i) * c_w, c_w), c_w)]
-        return load(src, dst, wld.at[i, c])
+        return load(src, dst, wld.at[c])
+
+    def gu_wait(c):
+        both = wgu.at[:, pl.ds(pl.multiple_of(2 * c * c_w, 2 * c_w), 2 * c_w)]
+        load(wg_h.at[:, pl.ds(0, 2 * c_w)], both, wld.at[c]).wait()
 
     wd_load = load(wd_h, wd, ld.at[5])
 
@@ -115,7 +117,10 @@
     sq_part = jnp.sum(x_f * x_f, axis=-1, keepdims=True)
 
     def qkv_step(i):
-        wq_load(i).wait()
+        @pl.when(i == 0)
+        def _():
+            wq_load.wait()
+
         cols = pl.ds(pl.multiple_of(i * 1024, 1024), 1024)
         y32[0] += nt_dot(dq[:, cols], wq[:, cols])
 
@@ -190,7 +195,7 @@
     gu_load_start(5)
     inv1 = lax.rsqrt(sq / d_model + NORM_EPS)
     n1[...] = (x_s[...].astype(F32) * inv1 * g1[...]).astype(BF)
-    n1_out = load(n1, n1_o, out_sem.at[0])
+    n1_out = load(n1, n1_o, ld.at[0])
     n1_out.start()
     acc[...] = jnp.zeros_like(acc)
 
@@ -248,7 +253,7 @@
         first, count = f_parts[n % 2] if n < 4 else (0, nc)
         ref = fb.at[xnb_q if n in (2, 3) else own_q, pl.ds(first, count)]
         return pltpu.make_async_remote_copy(
-            src_ref=ref, dst_ref=ref, send_sem=f_sem.at[n, 0], recv_sem=f_sem.at[n, 1],
+            src_ref=ref, dst_ref=ref, send_sem=f_sem.at[5], recv_sem=f_sem.at[n],
             device_id=xnb if n < 2 else pair, device_id_type=MESH_ID,
         )
 
@@ -260,7 +265,6 @@
 
         def direct(c):
             return c >= nc - DIRECT_LAST if ph == 0 else c < DIRECT_FIRST
-
 
         def reduce_pair(c):
             slot = lax.rem(c, 2)
@@ -293,8 +297,7 @@
 
                 @pl.when(t == 1)
                 def _():
-                    for i in range(qn):
-                        wq_load(i).start()
+                    wq_load.start()
 
                 @pl.when(t == 2)
                 def _():
@@ -380,8 +383,7 @@
 
     def gu_partial(c, which):
         if which is not core:
-            gu_load(0, c).wait()
-            gu_load(1, c).wait()
+            gu_wait(c)
         slot = lax.rem(c, 2)
         if which is None:
             prod = nn_dot(n1[...], wgu[:, pl.ds(pl.multiple_of(2 * c * c_w, 2 * c_w), 2 * c_w)])
@@ -424,7 +426,7 @@
     pipeline(0, gu_partial, act_forward, down_dot)
     wait_sends(0)
     f_copy(4).start()
-    a_out = load(a_f, a_o, out_sem.at[1])
+    a_out = load(a_f, a_o, ld.at[1])
     a_out.start()
 
     small[3].wait()
@@ -452,7 +454,7 @@
     eb[...] = e_val.astype(BF)
     n2[...] = (x2_s[...].astype(F32) * inv2 * g2[...]).astype(BF)
     dg_s[0:1, :] = jnp.sum(acc[...] * x2_s[...].astype(F32) * inv2, axis=0, keepdims=True)
-    outs = [load(eb, eb_o, out_sem.at[2]), load(n2, n2_o, out_sem.at[3])]
+    outs = [load(eb, eb_o, ld.at[2]), load(n2, n2_o, ld.at[3])]
     for cp in outs:
         cp.start()
     acc[...] = jnp.zeros_like(acc)
@@ -499,32 +501,31 @@
                 y_send(2, j)
 
     pipeline(1, da_partial, act_backward, dn1_dot)
-    dgu_out = load(dgu_f, dgu_o, out_sem.at[4])
+    dgu_out = load(dgu_f, dgu_o, ld.at[4])
 
     stat_send(2, [jnp.sum(g1[...] * acc[...] * x_s[...].astype(F32), axis=-1, keepdims=True)], PEERS)
     dgu_out.start()
     wait_sends(1)
-    for n in range(5):
-        f_copy(n).wait_send()
+    sent = fb.at[pl.ds(0, 3)]
+    pltpu.make_async_remote_copy(
+        src_ref=sent, dst_ref=sent, send_sem=f_sem.at[5], recv_sem=f_sem.at[0], device_id=pair, device_id_type=MESH_ID
+    ).wait_send()
     for j in range(YB):
         acc[:, y_cols(j)] = y_sum(2, j)
     y_wait_send(1)
     y_wait_send(2)
-    with jax.named_scope("fin0"):
-      dg_s[1:2, :] = jnp.sum(acc[...] * x_s[...].astype(F32) * inv1, axis=0, keepdims=True)
+    dg_s[1:2, :] = jnp.sum(acc[...] * x_s[...].astype(F32) * inv1, axis=0, keepdims=True)
     with jax.named_scope("stat2"):
         (dot1,) = stat_recv(2, 1, PEERS)
-    with jax.named_scope("fin1"):
-      dz1 = inv1 * (g1[...] * acc[...]) - x_s[...].astype(F32) * (inv1 * inv1 * inv1) * (dot1 / d_model)
-      dxin_s[...] = (e_s[...] + dz1).astype(BF)
+    dz1 = inv1 * (g1[...] * acc[...]) - x_s[...].astype(F32) * (inv1 * inv1 * inv1) * (dot1 / d_model)
+    dxin_s[...] = (e_s[...] + dz1).astype(BF)
     tail = [
-        load(dxin_s, dxin_o, out_sem.at[5]),
-        load(dg_s, dg_o, out_sem.at[6]),
+        load(dxin_s, dxin_o, ld.at[5]),
+        load(dg_s, dg_o, qld.at[0]),
     ]
     for cp in tail:
         cp.start()
-    with jax.named_scope("fin2"):
-      for cp in (n1_out, a_out, *outs, dgu_out, *tail):
+    for cp in (n1_out, a_out, *outs, dgu_out, *tail):
         cp.wait()
 
 
@@ -554,7 +555,7 @@
             vm(nc, 2, tok, quart, F32), vm(4, nc, 2, tok, quart, BF), vm(tok, ff, BF), vm(tok, ff, BF), vm(tok, 2 * ff, BF),
             vm(2, tok, hd, F32), vm(2, tok, hd, BF), vm(2, tok, hd, BF), vm(3, 8, 128, F32), vm(3, 8, 8, 128, F32),
             vm(tok, hd, BF), vm(8, hd, F32),
-            dma((6,)), dma((2, nc)), dma((qw // 1024,)), dma((7,)), dma((3, 2)), dma((3, YB + 1)), dma((5, nc)), dma((6,)), dma((5, 2)),
+            dma((6,)), dma((nc,)), dma((1,)), dma((3, 2)), dma((3, YB + 1)), dma((5, nc)), dma((6,)), dma((6,)),
         ],
         compiler_params=pltpu.CompilerParams(
             collective_id=0, has_side_effects=True, vmem_limit_bytes=VMEM_LIMIT
@@ -564,7 +565,7 @@
 
 
 TILE = CHUNK
-SLOTS = 2
+SLOTS = 3
 
 
 def grad_kernel(
@@ -620,9 +621,8 @@
     def step(i, carry):
         slot = lax.rem(i, SLOTS)
 
-        with jax.named_scope("b_wait"):
-          @pl.when(i >= SLOTS)
-          def _():
+        @pl.when(i >= SLOTS)
+        def _():
             for kind in (1, 2, 3):
                 out_copy(kind, i - SLOTS).wait()
 
@@ -637,10 +637,9 @@
     lax.fori_loop(0, nt, step, 0)
     for cp in finals:
         cp.wait()
-    with jax.named_scope("b_end"):
-     for i in range(nq - SLOTS, nq):
+    for i in range(max(nq - SLOTS, 0), nq):
         out_copy(0, i).wait()
-     for i in range(nt - SLOTS, nt):
+    for i in range(nt - SLOTS, nt):
         for kind in (1, 2, 3):
             out_copy(kind, i).wait()
 

time: 81.9 us -> 80.5 us (0.983)
  Pallas kernels: 81.1 us -> 79.8 us
where the time goes in v5:
time: 80.5 us; the launch traced here: 80.4 us
  Pallas kernels  79.8 us (99%)
    pallas_call x1, Pallas kernels, comm_call(): pl.pallas_call(functools.partial(comm_kernel, (tok, hd, ff, qw)), out_sha...  61.5 us
    pallas_call x1, Pallas kernels, grad_call(): pl.pallas_call(functools.partial(grad_kernel, (hd, ff, qw)), out_shape=(o...  18.2 us

profile of v5, /device:TPU:0, one launch (start us, length us, event | category | flops | bytes accessed | tf_op | source)
XLA Modules:
  0.0 80.4 jit_solution(11722246307134571148)
XLA Ops:
  0.6 61.5 %block_comm.1 = (bf16[64,1024]{1,0:T(8,128)(2,1)}, bf16[64,1024]{1,0:T(8,128)(2,1)}, bf16[64,1024]{1,0:T(8,128)(2,1)}, bf16[64,7168]{1,0:T(8,128)(2,1)}, bf16[64...) custom-call(bf16[64,1024]{1,0:T(8,128)(2,1)} %x_h.1, f32[1,1024]{1,0:T(1,128)} %bitcast.4, ...), custom_call_target="tpu_custom_call" | custom-call | tf_op jit(solution)/shard_map/block_comm/pallas_call | solution.py:541
  62.2 18.2 %weight_grads.1 = (bf16[1024,7168]{1,0:T(8,128)(2,1)}, bf16[1024,7168]{1,0:T(8,128)(2,1)}, bf16[7168,1024]{1,0:T(8,128)(2,1)}, bf16[1024,3072]{1,0:T(8,128)(2,1)...) custom-call(bf16[64,1024]{1,0:T(8,128)(2,1)} %get-tuple-element.21.n1_h, ...), custom_call_target="tpu_custom_call" | custom-call | tf_op jit(solution)/shard_map/weight_grads/pallas_call | solution.py:652

commit v6 on v5

--- a/solution.py
+++ b/solution.py
@@ -322,19 +322,10 @@
 
                 with jax.named_scope(f"part{ph}"):
 
-                    @pl.when(c == 0)
-                    def _():
-                        partial(c, 1 - core)
-                        pair_copy(ph, c).start()
-                        partial(c, core)
-                        reduce_pair(c)
-
-                    @pl.when(c > 0)
-                    def _():
-                        partial(c, None)
-                        pair_copy(ph, c).start()
-
-            @pl.when((t > lag_pair) & (t < nc + lag_pair))
+                    partial(c)
+                    pair_copy(ph, c).start()
+
+            @pl.when((t >= lag_pair) & (t < nc + lag_pair))
             def _():
                 reduce_pair(t - lag_pair)
 
@@ -381,19 +372,13 @@
 
         lax.fori_loop(0, nc + lag_dot, step, 0)
 
-    def gu_partial(c, which):
-        if which is not core:
-            gu_wait(c)
+    def gu_partial(c):
+        gu_wait(c)
         slot = lax.rem(c, 2)
-        if which is None:
-            prod = nn_dot(n1[...], wgu[:, pl.ds(pl.multiple_of(2 * c * c_w, 2 * c_w), 2 * c_w)])
-            for i in range(2):
-                part[slot, 0, i] = prod[:, i * c_w : i * c_w + half]
-                part[slot, 1, i] = prod[:, i * c_w + half : (i + 1) * c_w]
-        else:
-            for i in range(2):
-                cols = pl.ds(pl.multiple_of((2 * c + i) * c_w + which * half, half), half)
-                part[slot, which, i] = nn_dot(n1[...], wgu[:, cols])
+        prod = nn_dot(n1[...], wgu[:, pl.ds(pl.multiple_of(2 * c * c_w, 2 * c_w), 2 * c_w)])
+        for i in range(2):
+            part[slot, 0, i] = prod[:, i * c_w : i * c_w + half]
+            part[slot, 1, i] = prod[:, i * c_w + half : (i + 1) * c_w]
 
     def act_forward(c):
         gate = gu[c, 0] + xr[c, 0].astype(F32)
@@ -459,14 +444,11 @@
         cp.start()
     acc[...] = jnp.zeros_like(acc)
 
-    def da_partial(c, which):
+    def da_partial(c):
         slot = lax.rem(c, 2)
-        if which is None:
-            prod = nt_dot(eb[...], wd[pl.ds(pl.multiple_of(c * c_w, c_w), c_w), :])
-            part[slot, 0, 0] = prod[:, :half]
-            part[slot, 1, 0] = prod[:, half:]
-        else:
-            part[slot, which, 0] = nt_dot(eb[...], wd[pl.ds(pl.multiple_of(c * c_w + which * half, half), half), :])
+        prod = nt_dot(eb[...], wd[pl.ds(pl.multiple_of(c * c_w, c_w), c_w), :])
+        part[slot, 0, 0] = prod[:, :half]
+        part[slot, 1, 0] = prod[:, half:]
 
     def act_backward(c):
         cols = pl.ds(pl.multiple_of(c * c_w + own_q * quart, quart), quart)

time: 80.5 us -> 79.7 us (0.990)
  Pallas kernels: 79.8 us -> 78.9 us
    pallas_call x1, Pallas kernels: 61.5 us -> 60.7 us  [comm_call(): pl.pallas_call(functools.partial(comm_kernel, (tok, hd, ff, qw)), out_sha...]
where the time goes in v6:
time: 79.7 us; the launch traced here: 79.6 us
  Pallas kernels  78.9 us (99%)
    pallas_call x1, Pallas kernels, comm_call(): pl.pallas_call(functools.partial(comm_kernel, (tok, hd, ff, qw)), out_sha...  60.7 us
    pallas_call x1, Pallas kernels, grad_call(): pl.pallas_call(functools.partial(grad_kernel, (hd, ff, qw)), out_shape=(o...  18.2 us

profile of v6, /device:TPU:0, one launch (start us, length us, event | category | flops | bytes accessed | tf_op | source)
XLA Modules:
  0.0 79.6 jit_solution(15926216238304986924)
XLA Ops:
  0.6 60.7 %block_comm.1 = (bf16[64,1024]{1,0:T(8,128)(2,1)}, bf16[64,1024]{1,0:T(8,128)(2,1)}, bf16[64,1024]{1,0:T(8,128)(2,1)}, bf16[64,7168]{1,0:T(8,128)(2,1)}, bf16[64...) custom-call(bf16[64,1024]{1,0:T(8,128)(2,1)} %x_h.1, f32[1,1024]{1,0:T(1,128)} %bitcast.4, ...), custom_call_target="tpu_custom_call" | custom-call | tf_op jit(solution)/shard_map/block_comm/pallas_call | solution.py:523
  61.3 18.2 %weight_grads.1 = (bf16[1024,7168]{1,0:T(8,128)(2,1)}, bf16[1024,7168]{1,0:T(8,128)(2,1)}, bf16[7168,1024]{1,0:T(8,128)(2,1)}, bf16[1024,3072]{1,0:T(8,128)(2,1)...) custom-call(bf16[64,1024]{1,0:T(8,128)(2,1)} %get-tuple-element.21.n1_h, ...), custom_call_target="tpu_custom_call" | custom-call | tf_op jit(solution)/shard_map/weight_grads/pallas_call | solution.py:634

commit v7 on v6

--- a/solution.py
+++ b/solution.py
@@ -336,8 +336,8 @@
                     x_copy(ph, c).wait_recv()
                 with jax.named_scope(f"act{ph}"):
                     activate(c)
+                g_copy(ph, c, GP).start()
                 g_copy(ph, c, GX).start()
-                g_copy(ph, c, GP).start()
 
                 @pl.when(direct(c))
                 def _():
@@ -429,19 +429,17 @@
         dot_two += jnp.sum(g2[:, cols] * acc[:, cols] * x2, axis=-1, keepdims=True)
     stat_send(1, [sq_two, dot_two])
     f_copy(1).start()
+    acc[...] = g2[...] * acc[...]
     with jax.named_scope("stat1"):
         sq2, dot2 = stat_recv(1, 2)
     inv2 = lax.rsqrt(sq2 / d_model + NORM_EPS)
     x2 = x2_s[...].astype(F32)
-    dz2 = inv2 * (g2[...] * acc[...]) - x2 * (inv2 * inv2 * inv2) * (dot2 / d_model)
+    dz2 = inv2 * acc[...] - x2 * (inv2 * inv2 * inv2) * (dot2 / d_model)
     e_val = dx_s[...].astype(F32) + dz2
     e_s[...] = e_val
     eb[...] = e_val.astype(BF)
-    n2[...] = (x2_s[...].astype(F32) * inv2 * g2[...]).astype(BF)
-    dg_s[0:1, :] = jnp.sum(acc[...] * x2_s[...].astype(F32) * inv2, axis=0, keepdims=True)
-    outs = [load(eb, eb_o, ld.at[2]), load(n2, n2_o, ld.at[3])]
-    for cp in outs:
-        cp.start()
+    eb_out = load(eb, eb_o, ld.at[2])
+    eb_out.start()
     acc[...] = jnp.zeros_like(acc)
 
     def da_partial(c):
@@ -488,6 +486,11 @@
     stat_send(2, [jnp.sum(g1[...] * acc[...] * x_s[...].astype(F32), axis=-1, keepdims=True)], PEERS)
     dgu_out.start()
     wait_sends(1)
+    xr2_f = x2_s[...].astype(F32) * inv2
+    n2[...] = (xr2_f * g2[...]).astype(BF)
+    dg_s[0:1, :] = jnp.sum((y32[0] + y32[1]) * xr2_f, axis=0, keepdims=True)
+    n2_out = load(n2, n2_o, ld.at[3])
+    n2_out.start()
     sent = fb.at[pl.ds(0, 3)]
     pltpu.make_async_remote_copy(
         src_ref=sent, dst_ref=sent, send_sem=f_sem.at[5], recv_sem=f_sem.at[0], device_id=pair, device_id_type=MESH_ID
@@ -507,7 +510,7 @@
     ]
     for cp in tail:
         cp.start()
-    for cp in (n1_out, a_out, *outs, dgu_out, *tail):
+    for cp in (n1_out, a_out, eb_out, n2_out, dgu_out, *tail):
         cp.wait()
 
 

time: 79.7 us -> 79.6 us (level)
  no operation moved by 1% of the time
where the time goes in v7:
time: 79.6 us; the launch traced here: 79.5 us
  Pallas kernels  78.9 us (99%)
    pallas_call x1, Pallas kernels, comm_call(): pl.pallas_call(functools.partial(comm_kernel, (tok, hd, ff, qw)), out_sha...  60.6 us
    pallas_call x1, Pallas kernels, grad_call(): pl.pallas_call(functools.partial(grad_kernel, (hd, ff, qw)), out_shape=(o...  18.2 us

profile of v7, /device:TPU:0, one launch (start us, length us, event | category | flops | bytes accessed | tf_op | source)
XLA Modules:
  0.0 79.5 jit_solution(7802331650406985888)
XLA Ops:
  0.6 60.6 %block_comm.1 = (bf16[64,1024]{1,0:T(8,128)(2,1)}, bf16[64,1024]{1,0:T(8,128)(2,1)}, bf16[64,1024]{1,0:T(8,128)(2,1)}, bf16[64,7168]{1,0:T(8,128)(2,1)}, bf16[64...) custom-call(bf16[64,1024]{1,0:T(8,128)(2,1)} %x_h.1, f32[1,1024]{1,0:T(1,128)} %bitcast.4, ...), custom_call_target="tpu_custom_call" | custom-call | tf_op jit(solution)/shard_map/block_comm/pallas_call | solution.py:526
  61.3 18.2 %weight_grads.1 = (bf16[1024,7168]{1,0:T(8,128)(2,1)}, bf16[1024,7168]{1,0:T(8,128)(2,1)}, bf16[7168,1024]{1,0:T(8,128)(2,1)}, bf16[1024,3072]{1,0:T(8,128)(2,1)...) custom-call(bf16[64,1024]{1,0:T(8,128)(2,1)} %get-tuple-element.21.n1_h, ...), custom_call_target="tpu_custom_call" | custom-call | tf_op jit(solution)/shard_map/weight_grads/pallas_call | solution.py:637

commit v8 on v7

--- a/solution.py
+++ b/solution.py
@@ -491,6 +491,8 @@
     dg_s[0:1, :] = jnp.sum((y32[0] + y32[1]) * xr2_f, axis=0, keepdims=True)
     n2_out = load(n2, n2_o, ld.at[3])
     n2_out.start()
+    y32[0] = x_s[...].astype(F32) * (inv1 * inv1 * inv1)
+    y32[1] = inv1 * g1[...]
     sent = fb.at[pl.ds(0, 3)]
     pltpu.make_async_remote_copy(
         src_ref=sent, dst_ref=sent, send_sem=f_sem.at[5], recv_sem=f_sem.at[0], device_id=pair, device_id_type=MESH_ID
@@ -502,7 +504,7 @@
     dg_s[1:2, :] = jnp.sum(acc[...] * x_s[...].astype(F32) * inv1, axis=0, keepdims=True)
     with jax.named_scope("stat2"):
         (dot1,) = stat_recv(2, 1, PEERS)
-    dz1 = inv1 * (g1[...] * acc[...]) - x_s[...].astype(F32) * (inv1 * inv1 * inv1) * (dot1 / d_model)
+    dz1 = y32[1] * acc[...] - y32[0] * (dot1 / d_model)
     dxin_s[...] = (e_s[...] + dz1).astype(BF)
     tail = [
         load(dxin_s, dxin_o, ld.at[5]),

time: 79.6 us -> 79.6 us (level)
  no operation moved by 1% of the time
where the time goes in v8:
time: 79.6 us; the launch traced here: 79.5 us
  Pallas kernels  78.9 us (99%)
    pallas_call x1, Pallas kernels, comm_call(): pl.pallas_call(functools.partial(comm_kernel, (tok, hd, ff, qw)), out_sha...  60.6 us
    pallas_call x1, Pallas kernels, grad_call(): pl.pallas_call(functools.partial(grad_kernel, (hd, ff, qw)), out_shape=(o...  18.2 us

profile of v8, /device:TPU:0, one launch (start us, length us, event | category | flops | bytes accessed | tf_op | source)
XLA Modules:
  0.0 79.5 jit_solution(16108558397509739733)
XLA Ops:
  0.6 60.6 %block_comm.1 = (bf16[64,1024]{1,0:T(8,128)(2,1)}, bf16[64,1024]{1,0:T(8,128)(2,1)}, bf16[64,1024]{1,0:T(8,128)(2,1)}, bf16[64,7168]{1,0:T(8,128)(2,1)}, bf16[64...) custom-call(bf16[64,1024]{1,0:T(8,128)(2,1)} %x_h.1, f32[1,1024]{1,0:T(1,128)} %bitcast.4, ...), custom_call_target="tpu_custom_call" | custom-call | tf_op jit(solution)/shard_map/block_comm/pallas_call | solution.py:528
  61.3 18.2 %weight_grads.1 = (bf16[1024,7168]{1,0:T(8,128)(2,1)}, bf16[1024,7168]{1,0:T(8,128)(2,1)}, bf16[7168,1024]{1,0:T(8,128)(2,1)}, bf16[1024,3072]{1,0:T(8,128)(2,1)...) custom-call(bf16[64,1024]{1,0:T(8,128)(2,1)} %get-tuple-element.21.n1_h, ...), custom_call_target="tpu_custom_call" | custom-call | tf_op jit(solution)/shard_map/weight_grads/pallas_call | solution.py:639
